TPU v7x, 128 devices: a whole 4x4x4 slice. The times are simulated.
128 devices in a mesh: dp: 4 (over x), section: 2 (over core), tensor: 16 (over z, y).
Axes of the slice: x: 4, y: 4, z: 4, core: 2. Of those that a mesh axis runs over, the one named last changes fastest.
Arguments:
- in_delta: bfloat16 [8, 1024, 4096], P(None, ('dp', 'tensor')), may hold values from -12 to 12
- weight: bfloat16 [2, 4096, 4096], P('section', 'tensor'), may hold values from -0.09375 to 0.09375
- cache_codes: int32 [2, 2, 8, 1024, 4096], P('section', None, None, ('dp', 'tensor')), may hold values from -7 to 7, as said below
- cache_scales: float32 [2, 2, 8, 4, 32], P('section', None, None, 'dp'), may hold values from 0.2 to 6, as said below
- cotangent: bfloat16 [8, 1024, 4096], P(None, ('dp', 'tensor')), may hold values from -16 to 16
Outputs:
- out_deltas: bfloat16 [2, 8, 1024, 4096], P('section', None, ('dp', 'tensor'))
- grad_in: bfloat16 [2, 8, 1024, 4096], P('section', None, ('dp', 'tensor'))
- weight_grad: float32 [2, 4096, 4096], P('section', 'tensor', 'dp')
Inputs may be any that keep to these rules, and one draw needn't show every extreme that they name: cache_codes[s, 1] equals cache_codes[s + 1, 0]: the buffer of a boundary between two segments is held by both. cache_scales[s, 1] equals cache_scales[s + 1, 0].
All inputs are finite; a program needn't handle non-finite values. Where the computation divides by a largest or mean magnitude, that divisor is 1e-20 or more.
Results may differ from a plain program's by a relative error of at most 0.013.
Values may be sent and summed in bfloat16 or wider, within the bound.
No kernel may reach another device: no remote copies, remote signals or barrier semaphores. Data moves between devices by JAX's collectives and lax.ppermute only.
A program may use at most 128 MiB of HBM per device.

v0:
```python
import functools

import jax
import jax.numpy as jnp
from jax import lax
from jax.experimental import pallas as pl
from jax.experimental.pallas import tpu as pltpu
from jax.sharding import Mesh
from jax.sharding import PartitionSpec as P


TENSOR = ("tensor_0", "tensor_1")
CHIP = ("section", "tensor_0", "tensor_1")
DP_TENSOR = ("dp", "tensor_0", "tensor_1")
SIDE = 4
BLOCK = 128
PER = 8
STEPS = 2
VMEM_LIMIT = 24 * 1024 * 1024

code_levels = 7.0
softness = 0.8
two_pi = 6.283185307179586
epsilon = 1e-06

SINE = (25.13274118, -64.8358279, 67.07681018, -38.49815464, 14.06107271, -3.181409966)


def on_z(s, phase, along):
    return ((s + phase) % 2 == 0) == (along == "rows")


def position(s, z, y):
    return (s * SIDE + z) * SIDE + y


def shift(value, phase, along, steps):
    pairs = []
    for s in range(2):
        for z in range(SIDE):
            for y in range(SIDE):
                if on_z(s, phase, along):
                    target = position(s, (z + steps) % SIDE, y)
                else:
                    target = position(s, z, (y + steps) % SIDE)
                pairs.append((position(s, z, y), target))
    return lax.ppermute(value, CHIP, pairs)


def ring(value, axis, steps):
    return lax.ppermute(value, axis, [(i, (i + steps) % SIDE) for i in range(SIDE)])


def crossed_over(value):
    return lax.ppermute(value, "section", [(0, 1), (1, 0)])


def lanes(block):
    return slice(block * BLOCK, (block + 1) * BLOCK)


def f32(value):
    return value.astype(jnp.float32)


def call(body, ids, grid, inputs, in_specs, shapes, out_specs, scratch=(), flops=0, aliases=None):
    cost = pl.CostEstimate(flops=flops or 20_000_000, bytes_accessed=8_000_000, transcendentals=0)
    return pl.pallas_call(
        body,
        grid_spec=pltpu.PrefetchScalarGridSpec(
            num_scalar_prefetch=1,
            grid=grid,
            in_specs=in_specs,
            out_specs=out_specs,
            scratch_shapes=scratch,
        ),
        out_shape=shapes,
        cost_estimate=cost,
        compiler_params=pltpu.CompilerParams(vmem_limit_bytes=VMEM_LIMIT),
        input_output_aliases=aliases or {},
    )(ids, *inputs)


def root_mean(squares, width):
    return lax.rsqrt(jnp.sum(squares, axis=-1, keepdims=True) * (1.0 / width) + epsilon)


def column(place, steps, inner):
    n = lax.rem(place + steps + SIDE, SIDE)
    return pl.ds(pl.multiple_of(n * PER * BLOCK + inner * BLOCK, BLOCK), BLOCK)


def scale_at(scales, slot, micro, place, steps, inner):
    n = lax.rem(place + steps + SIDE, SIDE)
    return scales[slot, micro, n * PER + inner] / code_levels


def each_micro(count, step):
    lax.fori_loop(0, count, lambda m, _: (step(m), None)[1], None)


def first_body(ids, scales, near, arriving, cot, *refs):
    outs, hidden = refs[:SIDE], refs[SIDE]
    count, rows, width = arriving.shape
    start = pl.program_id(0) * count

    @pl.when(ids[0] == 0)
    def _():
        def step(m):
            i = start + m
            at_rows = pl.ds(pl.multiple_of(m * rows, rows), rows)
            squares = jnp.zeros((rows, BLOCK), jnp.float32)
            for block in range(width // BLOCK):
                at = lanes(block)
                value = f32(near[0, m, :, at]) * (scales[0, i, block] / code_levels) + f32(
                    arriving[m, :, at]
                )
                hidden[:, at] = value
                squares = squares + value * value
            inverse = root_mean(squares, width)
            for k in range(SIDE):
                for inner in range(PER):
                    normed = hidden[:, column(ids[1], k, inner)] * inverse
                    outs[k][at_rows, lanes(inner)] = normed.astype(jnp.bfloat16)

        each_micro(count, step)

    @pl.when(ids[0] != 0)
    def _():
        def step(m):
            at_rows = pl.ds(pl.multiple_of(m * rows, rows), rows)
            for k in range(SIDE):
                for inner in range(PER):
                    outs[k][at_rows, lanes(inner)] = cot[m, :, column(ids[1], k, inner)]

        each_micro(count, step)


def first_side_body(ids, scales, near, far, arriving, *offsets):
    count, rows, _ = arriving.shape
    start = pl.program_id(0) * count

    @pl.when(ids[0] == 0)
    def _():
        def step(m):
            i = start + m
            at_rows = pl.ds(pl.multiple_of(m * rows, rows), rows)
            for j in range(SIDE):
                for inner in range(PER):
                    at = column(ids[2], j, inner)
                    hidden = f32(near[0, m, :, at]) * scale_at(
                        scales, 0, i, ids[2], j, inner
                    ) + f32(arriving[m, :, at])
                    behind = f32(far[0, m, :, at]) * scale_at(scales, 1, i, ids[2], j, inner)
                    offsets[j][at_rows, lanes(inner)] = (hidden - behind).astype(jnp.bfloat16)

        each_micro(count, step)


def tile(n, size):
    return pl.ds(pl.multiple_of(n * size, size), size)


def multiply(phase, ids, read, matrix, store):
    part = matrix.shape[0] // SIDE

    @pl.when(ids[0] == phase)
    def _():
        def step(n):
            cols = tile(n, part)
            store(jnp.dot(read(), matrix[:, cols], preferred_element_type=jnp.float32), cols)

        each_micro(SIDE, step)

    @pl.when(ids[0] != phase)
    def _():
        def step(n):
            cols = tile(n, part)
            product = lax.dot_general(
                read(), matrix[cols, :], (((1,), (1,)), ((), ())), preferred_element_type=jnp.float32
            )
            store(product, cols)

        each_micro(SIDE, step)


def early_body(phase, ids, p0, p1, p3, matrix, *outs):
    for j, group in ((0, p0), (1, p1), (3, p3)):
        def read(group=group):
            return group[...].reshape(-1, group.shape[-1])

        def store(product, cols, j=j):
            count = product.shape[0] // SIDE
            for k in range(SIDE):
                outs[k][j, :, cols] = product[k * count : (k + 1) * count].astype(jnp.bfloat16)

        multiply(phase, ids, read, matrix, store)


def late_body(phase, ids, low, high, matrix, *refs):
    outs = refs[SIDE:]

    def read():
        return jnp.concatenate([low[0], low[1], high[0], high[1]], axis=0)

    def store(product, cols):
        count = product.shape[0] // SIDE
        for k in range(SIDE):
            outs[k][0, :, cols] = product[k * count : (k + 1) * count].astype(jnp.bfloat16)

    multiply(phase, ids, read, matrix, store)


def combine_body(phase, ids, z0, z1, z2, z3, o0, o1, o2, o3, v0, v1, v2, v3, peak):
    offsets, outs = (o0, o1, o2, o3), (v0, v1, v2, v3)
    count = peak.shape[0]
    rows = z0.shape[1] // count
    forward = ids[0] == phase

    def step(m):
        at = pl.ds(pl.multiple_of(m * rows, rows), rows)
        for inner in range(PER):
            cols = lanes(inner)
            best = jnp.zeros((rows, BLOCK), jnp.float32)
            for j in range(SIDE):
                value = (f32(z0[j, at, cols]) + f32(z1[j, at, cols])) + (
                    f32(z2[j, at, cols]) + f32(z3[j, at, cols])
                )
                value = value + jnp.where(forward, f32(offsets[j][at, cols]), 0.0)
                outs[j][at, cols] = value.astype(jnp.bfloat16)
                best = jnp.maximum(best, jnp.abs(value))
            best = jnp.max(jnp.max(best, axis=0, keepdims=True), axis=1, keepdims=True)
            peak[m, :, cols] = jnp.broadcast_to(best, (1, BLOCK))

    each_micro(count, step)


def softened(delta, columns):
    spread = columns + epsilon
    level = delta * (code_levels / spread)
    part = level - jnp.round(level)
    square = part * part
    poly = jnp.full_like(square, SINE[-1])
    for coefficient in SINE[-2::-1]:
        poly = poly * square + coefficient
    sine = part * (0.25 - square) * poly
    smooth = level - (softness / two_pi) * sine
    return (smooth * (spread / code_levels)).astype(jnp.bfloat16)


def middle_body(ids, scales, *refs):
    own, other = refs[:SIDE], refs[SIDE : 2 * SIDE]
    own_peaks, other_peaks, between, cot = refs[2 * SIDE : 2 * SIDE + 4]
    outs = refs[2 * SIDE + 4 : 3 * SIDE + 4]
    sent, hidden, raw = refs[3 * SIDE + 4 :]
    count, rows, width = cot.shape
    start = pl.program_id(0) * count

    def step(m):
        i = start + m
        at_rows = pl.ds(pl.multiple_of(m * rows, rows), rows)

        def load(deltas, peaks, place):
            for j in range(SIDE):
                for inner in range(PER):
                    sent[m, :, column(place, j, inner)] = softened(
                        f32(deltas[j][at_rows, lanes(inner)]), peaks[j, i, :, lanes(inner)]
                    )

        def read(block, slot):
            at = lanes(block)
            return f32(between[0, m, :, at]) * (scales[slot, i, block] / code_levels) + f32(
                sent[m, :, at]
            )

        @pl.when(ids[0] == 0)
        def _():
            load(own, own_peaks, ids[2])
            for j in range(SIDE):
                for inner in range(PER):
                    raw[:, column(ids[1], j, inner)] = f32(other[j][at_rows, lanes(inner)])
            squares = jnp.zeros((rows, BLOCK), jnp.float32)
            crossed = jnp.zeros((rows, BLOCK), jnp.float32)
            for block in range(width // BLOCK):
                value = read(block, 1)
                hidden[:, lanes(block)] = value
                squares = squares + value * value
                crossed = crossed + value * raw[:, lanes(block)]
            inverse = root_mean(squares, width)
            mean = jnp.sum(crossed, axis=-1, keepdims=True) * (1.0 / width) * inverse * inverse
            for k in range(SIDE):
                for inner in range(PER):
                    at = column(ids[3], k, inner)
                    back = f32(cot[m, :, at]) + inverse * (raw[:, at] - hidden[:, at] * mean)
                    outs[k][at_rows, lanes(inner)] = back.astype(jnp.bfloat16)

        @pl.when(ids[0] != 0)
        def _():
            load(other, other_peaks, ids[1])
            squares = jnp.zeros((rows, BLOCK), jnp.float32)
            for block in range(width // BLOCK):
                value = read(block, 0)
                hidden[:, lanes(block)] = value
                squares = squares + value * value
            inverse = root_mean(squares, width)
            for k in range(SIDE):
                for inner in range(PER):
                    normed = hidden[:, column(ids[3], k, inner)] * inverse
                    outs[k][at_rows, lanes(inner)] = normed.astype(jnp.bfloat16)

    each_micro(count, step)


def middle_side_body(ids, scales, *refs):
    own, tokens = refs[:SIDE], refs[SIDE : 2 * SIDE]
    sent, near, far, cot = refs[2 * SIDE : 2 * SIDE + 4]
    offsets = refs[2 * SIDE + 4 : 3 * SIDE + 4]
    grads, hidden, raw = refs[3 * SIDE + 4 :]
    count, rows, width = cot.shape
    start = pl.program_id(0) * count

    @pl.when(ids[0] == 0)
    def _():
        def step(m):
            at_rows = pl.ds(pl.multiple_of(m * rows, rows), rows)
            for k in range(SIDE):
                for inner in range(PER):
                    at = column(ids[3], k, inner)
                    grads[m, :, at] = tokens[k][at_rows, lanes(inner)]

        each_micro(count, step)

    @pl.when(ids[0] != 0)
    def _():
        def step(m):
            i = start + m
            at_rows = pl.ds(pl.multiple_of(m * rows, rows), rows)
            for j in range(SIDE):
                for inner in range(PER):
                    raw[:, column(ids[2], j, inner)] = f32(own[j][at_rows, lanes(inner)])
            squares = jnp.zeros((rows, BLOCK), jnp.float32)
            crossed = jnp.zeros((rows, BLOCK), jnp.float32)
            for block in range(width // BLOCK):
                at = lanes(block)
                value = f32(near[0, m, :, at]) * (scales[0, i, block] / code_levels) + f32(
                    sent[m, :, at]
                )
                hidden[:, at] = value
                squares = squares + value * value
                crossed = crossed + value * raw[:, at]
            inverse = root_mean(squares, width)
            mean = jnp.sum(crossed, axis=-1, keepdims=True) * (1.0 / width) * inverse * inverse
            for block in range(width // BLOCK):
                at = lanes(block)
                back = f32(cot[m, :, at]) + inverse * (raw[:, at] - hidden[:, at] * mean)
                grads[m, :, at] = back.astype(jnp.bfloat16)
            for j in range(SIDE):
                for inner in range(PER):
                    at = column(ids[4], j, inner)
                    behind = f32(far[0, m, :, at]) * scale_at(scales, 1, i, ids[4], j, inner)
                    offsets[j][at_rows, lanes(inner)] = (hidden[:, at] - behind).astype(
                        jnp.bfloat16
                    )

        each_micro(count, step)


def last_body(ids, scales, r0, r1, r2, r3, peaks, near, arriving, upstream, sent, outs, grads, hidden, raw):
    result = (r0, r1, r2, r3)
    count, rows, width = arriving.shape
    start = pl.program_id(0) * count
    b = ids[4]

    @pl.when(ids[0] == 0)
    def _():
        def step(m):
            at_rows = pl.ds(pl.multiple_of(m * rows, rows), rows)
            for j in range(SIDE):
                for inner in range(PER):
                    raw[:, column(b, j, inner)] = f32(result[j][at_rows, lanes(inner)])
            squares = jnp.zeros((rows, BLOCK), jnp.float32)
            crossed = jnp.zeros((rows, BLOCK), jnp.float32)
            for block in range(width // BLOCK):
                at = lanes(block)
                value = f32(near[0, m, :, at]) * (
                    scales[0, start + m, block] / code_levels
                ) + f32(arriving[m, :, at])
                hidden[:, at] = value
                squares = squares + value * value
                crossed = crossed + value * raw[:, at]
            inverse = root_mean(squares, width)
            mean = jnp.sum(crossed, axis=-1, keepdims=True) * (1.0 / width) * inverse
            for block in range(width // BLOCK):
                at = lanes(block)
                unrounded = hidden[:, at] * inverse
                back = f32(upstream[m, :, at]) + inverse * (raw[:, at] - unrounded * mean)
                grads[m, :, at] = back.astype(jnp.bfloat16)

        each_micro(count, step)
        outs[...] = sent[...]

    @pl.when(ids[0] != 0)
    def _():
        def step(m):
            at_rows = pl.ds(pl.multiple_of(m * rows, rows), rows)
            for j in range(SIDE):
                for inner in range(PER):
                    outs[m, :, column(b, j, inner)] = softened(
                        f32(result[j][at_rows, lanes(inner)]),
                        peaks[j, start + m, :, lanes(inner)],
                    )

        each_micro(count, step)
        grads[...] = upstream[...]


def turn_body(ids, p0, p1, low, high, p3, out):
    rows = p0.shape[1]
    for i in range(SIDE):
        for j in range(SIDE):
            if j == 2:
                source = low[i] if i < 2 else high[i - 2]
            else:
                source = (p0, p1, None, p3)[j][i]
            at = (i * SIDE + j) * rows
            out[:, at : at + rows] = source.T


def gradient_body(ids, left, p0, p1, low, high, p3, *outs):
    span = left.shape[0]
    part = span // SIDE
    depth = left.shape[1] // SIDE

    def product(rows, columns):
        total = None
        for i, groups in enumerate(((p0,), (p1,), (low, high), (p3,))):
            right = jnp.concatenate(
                [group[j, :, columns] for group in groups for j in range(group.shape[0])], axis=0
            )
            term = jnp.dot(
                left[rows, i * depth : (i + 1) * depth], right, preferred_element_type=jnp.float32
            )
            total = term if total is None else total + term
        return total.astype(jnp.bfloat16)

    for k in range(SIDE):
        mine = tile(lax.rem(ids[5] + k, SIDE), part)

        @pl.when(ids[0] == 0)
        def _():
            def step(n):
                outs[k][tile(n, part), :] = product(tile(n, part), mine)

            each_micro(SIDE, step)

        @pl.when(ids[0] != 0)
        def _():
            def step(n):
                outs[k][tile(n, part), :] = product(mine, tile(n, part)).T

            each_micro(SIDE, step)


def total_body(ids, q0, q1, q2, q3, *outs):
    part = q0.shape[1]
    for k in range(SIDE):
        at = tile(lax.rem(ids[6] + k, SIDE), part)
        total = (f32(q0[at, :]) + f32(q1[at, :])) + (f32(q2[at, :]) + f32(q3[at, :]))
        outs[k][...] = total.astype(jnp.bfloat16)


def choose_body(ids, r0, r1, r2, r3, *outs):
    for l in range(SIDE):
        k = lax.rem(ids[6] - ids[5] - l + 2 * SIDE, SIDE)
        for at, source in enumerate((r0, r1, r2, r3)):
            @pl.when(k == at)
            def _():
                outs[l][...] = source[...]


def pass_body(ids, *refs):
    half = len(refs) // 2
    for source, target in zip(refs[:half], refs[half:]):
        target[...] = source[...]


def assemble_body(ids, a0, b0, a1, b1, out):
    depth = a0.shape[1]
    odd = lax.rem(ids[5], 2)
    for k in range(SIDE):
        row = lax.rem(ids[6] - k + SIDE, SIDE) * SIDE
        for at, group in ((2 * odd, a0), (2 * odd + 1, b0), (2 - 2 * odd, a1), (3 - 2 * odd, b1)):
            out[tile(row + at, depth), :] = group[k]


def finish_body(ids, f0, f1, f2, f3, out):
    part = f0.shape[1]
    for l, piece in enumerate((f0, f1, f2, f3)):
        out[:, tile(lax.rem(ids[5] - l + SIDE, SIDE), part)] = f32(piece[...])


def local(in_delta, weight, cache_codes, cache_scales, cotangent):
    s = lax.axis_index("section")
    z = lax.axis_index("tensor_0")
    y = lax.axis_index("tensor_1")
    x = lax.axis_index("dp")
    micro_count, local_rows, width = in_delta.shape
    span = width // SIDE
    bf16, single = jnp.bfloat16, jnp.float32
    here = jnp.where(s == 0, z, y)
    there = jnp.where(s == 0, y, z)
    ids = jnp.stack([s, here, there, there, here, x, y]).astype(jnp.int32)

    count = micro_count // STEPS
    rows = micro_count * local_rows
    grid = (STEPS,)
    flat = (count, local_rows, width)
    in_smem = pl.BlockSpec(memory_space=pltpu.SMEM)
    piece = pl.BlockSpec((count * local_rows, span), lambda i, ids: (i, 0))
    piece_shape = jax.ShapeDtypeStruct((rows, span), bf16)
    whole = pl.BlockSpec(flat, lambda i, ids: (i, 0, 0))
    whole_shape = jax.ShapeDtypeStruct((micro_count, local_rows, width), bf16)
    work = [pltpu.VMEM((local_rows, width), single)]
    peak_shape = (micro_count, 1, span)
    peaks_spec = pl.BlockSpec((SIDE, *peak_shape), lambda i, ids: (0, 0, 0, 0))
    everything = pl.BlockSpec((SIDE, rows, span), lambda i, ids: (0, 0, 0))
    half = pl.BlockSpec((2, rows, span), lambda i, ids: (0, 0, 0))
    full_piece = pl.BlockSpec((rows, span), lambda i, ids: (0, 0))
    square = pl.BlockSpec((span, span), lambda i, ids: (0, 0))
    cut_shape = jax.ShapeDtypeStruct((SIDE, rows, span), bf16)
    codes, scales = cache_codes[0], cache_scales[0, :, :, 0, :]
    near = pl.BlockSpec((1, *flat), lambda i, ids: (0, i, 0, 0))
    far = pl.BlockSpec((1, *flat), lambda i, ids: (1, i, 0, 0))
    between = pl.BlockSpec((1, *flat), lambda i, ids: (1 - ids[0], i, 0, 0))

    depth = weight.shape[1] // 2

    def corner(k):
        return pl.BlockSpec(
            (depth, span), lambda i, ids: (lax.rem(ids[5], 2), lax.rem(ids[6] + k, SIDE))
        )

    halves = call(
        pass_body,
        ids,
        (1,),
        [weight[0]] * SIDE,
        [corner(k) for k in range(SIDE)],
        [jax.ShapeDtypeStruct((depth, span), bf16)] * SIDE,
        [pl.BlockSpec((depth, span), lambda i, ids: (0, 0))] * SIDE,
    )
    halves = [halves[0]] + [ring(halves[k], "tensor_1", k) for k in (1, 2, 3)]
    upper = jnp.stack([part[: depth // 2] for part in halves])
    lower = jnp.stack([part[depth // 2 :] for part in halves])
    block = call(
        assemble_body,
        ids,
        (1,),
        [upper, lower, ring(upper, "dp", 1), ring(lower, "dp", -1)],
        [pl.BlockSpec((SIDE, depth // 2, span), lambda i, ids: (0, 0, 0))] * SIDE,
        jax.ShapeDtypeStruct((span, span), bf16),
        square,
    )

    def spread_out(pieces, phase):
        mine = jnp.stack([pieces[0]] + [shift(pieces[k], phase, "rows", k) for k in (1, 2, 3)])
        after = shift(mine, phase, "columns", 1)
        before = shift(mine, phase, "columns", -1)
        low = shift(after[:2], phase, "columns", 1)
        high = shift(before[2:], phase, "columns", -1)
        return [mine, after, low, high, before]

    def moved(offsets, phase):
        return [offsets[0]] + [shift(offsets[j], phase, "columns", j) for j in (1, 2, 3)]

    def products(groups, phase):
        made = call(
            functools.partial(early_body, phase),
            ids,
            (1,),
            [groups[0], groups[1], groups[4], block],
            [everything] * 3 + [square],
            [cut_shape] * SIDE,
            [everything] * SIDE,
            flops=6 * SIDE * rows * span * span,
        )
        late = pl.BlockSpec((1, rows, span), lambda i, ids: (2, 0, 0))
        made = call(
            functools.partial(late_body, phase),
            ids,
            (1,),
            [groups[2], groups[3], block, *made],
            [half, half, square] + [pl.BlockSpec(memory_space=pl.ANY)] * SIDE,
            [cut_shape] * SIDE,
            [late] * SIDE,
            flops=2 * SIDE * rows * span * span,
            aliases={4 + k: k for k in range(SIDE)},
        )
        return [made[0]] + [shift(made[k], phase, "rows", -k) for k in (1, 2, 3)]

    def returned(arrived, offsets, phase):
        *sent, peak = call(
            functools.partial(combine_body, phase),
            ids,
            (1,),
            [*arrived, *offsets],
            [everything] * SIDE + [full_piece] * SIDE,
            [piece_shape] * SIDE + [jax.ShapeDtypeStruct(peak_shape, single)],
            [full_piece] * SIDE + [pl.BlockSpec(peak_shape, lambda i, ids: (0, 0, 0))],
        )
        for k, other in [(k, shift(peak, phase, "rows", k)) for k in (1, 2, 3)]:
            peak = jnp.maximum(peak, other)
        home = [sent[0]] + [shift(sent[j], phase, "columns", -j) for j in (1, 2, 3)]
        peaks = jnp.stack([peak] + [shift(peak, phase, "columns", -j) for j in (1, 2, 3)])
        return home, peaks

    tokens = call(
        first_body,
        ids,
        grid,
        [scales, codes, in_delta, cotangent],
        [in_smem, near, whole, whole],
        [piece_shape] * SIDE,
        [piece] * SIDE,
        work,
    )
    groups = spread_out(tokens, 0)
    offsets = call(
        first_side_body,
        ids,
        grid,
        [scales, codes, codes, in_delta],
        [in_smem, near, far, whole],
        [piece_shape] * SIDE,
        [piece] * SIDE,
    )
    offsets = moved(offsets, 0)
    own, own_peaks = returned(products(groups, 0), offsets, 0)
    other_peaks = crossed_over(own_peaks)
    other = [crossed_over(own[j]) for j in range(SIDE)]
    *tokens, sent = call(
        middle_body,
        ids,
        grid,
        [scales, *own, *other, own_peaks, other_peaks, codes, cotangent],
        [in_smem] + [piece] * (2 * SIDE) + [peaks_spec, peaks_spec, between, whole],
        [piece_shape] * SIDE + [whole_shape],
        [piece] * SIDE + [whole],
        work * 2,
    )
    groups_next = spread_out(tokens, 1)
    *offsets, upstream = call(
        middle_side_body,
        ids,
        grid,
        [scales, *own, *tokens, sent, codes, codes, cotangent],
        [in_smem] + [piece] * (2 * SIDE) + [whole, near, far, whole],
        [piece_shape] * SIDE + [whole_shape],
        [piece] * SIDE + [whole],
        work * 2,
    )
    offsets = moved(offsets, 1)
    result, peaks = returned(products(groups_next, 1), offsets, 1)
    outs, grads = call(
        last_body,
        ids,
        grid,
        [scales, *result, peaks, codes, in_delta, upstream, sent],
        [in_smem] + [piece] * SIDE + [peaks_spec, near, whole, whole, whole],
        [whole_shape, whole_shape],
        [whole, whole],
        work * 2,
    )

    total_rows = SIDE * SIDE * rows
    part = span // SIDE
    gathered_specs = [everything, everything, half, half, everything]
    tall = pl.BlockSpec((span, part), lambda i, ids: (0, 0))
    small = pl.BlockSpec((part, part), lambda i, ids: (0, 0))
    flipped = pl.BlockSpec((span, total_rows), lambda i, ids: (0, 0))
    left = call(
        turn_body,
        ids,
        (1,),
        groups,
        gathered_specs,
        jax.ShapeDtypeStruct((span, total_rows), bf16),
        flipped,
    )
    partials = call(
        gradient_body,
        ids,
        (1,),
        [left, *groups_next],
        [flipped, *gathered_specs],
        [jax.ShapeDtypeStruct((span, part), bf16)] * SIDE,
        [tall] * SIDE,
        flops=2 * total_rows * span * span,
    )
    arrived = [partials[0]] + [ring(partials[k], "dp", k) for k in (1, 2, 3)]
    pieces = call(
        total_body,
        ids,
        (1,),
        arrived,
        [tall] * SIDE,
        [jax.ShapeDtypeStruct((part, part), bf16)] * SIDE,
        [small] * SIDE,
    )
    pieces = [pieces[0]] + [ring(pieces[k], "tensor_1", k) for k in (1, 2, 3)]
    pieces = call(
        choose_body,
        ids,
        (1,),
        pieces,
        [small] * SIDE,
        [jax.ShapeDtypeStruct((part, part), bf16)] * SIDE,
        [small] * SIDE,
    )
    pieces = [pieces[0]] + [ring(pieces[k], "dp", k) for k in (1, 2, 3)]
    weight_grad = call(
        finish_body,
        ids,
        (1,),
        pieces,
        [small] * SIDE,
        jax.ShapeDtypeStruct((part, span), single),
        pl.BlockSpec((part, span), lambda i, ids: (0, 0)),
    )
    return outs[None], grads[None], weight_grad[None]


def solution(mesh):
    finer = Mesh(
        mesh.devices.reshape(mesh.shape["dp"], mesh.shape["section"], SIDE, SIDE),
        ("dp", "section", "tensor_0", "tensor_1"),
    )
    return jax.shard_map(
        local,
        mesh=finer,
        in_specs=(
            P(None, DP_TENSOR, None),
            P("section", TENSOR, None),
            P("section", None, None, DP_TENSOR, None),
            P("section", None, None, "dp", None),
            P(None, DP_TENSOR, None),
        ),
        out_specs=(
            P("section", None, DP_TENSOR, None),
            P("section", None, DP_TENSOR, None),
            P("section", TENSOR, "dp"),
        ),
        check_vma=False,
    )
```

profile of v0, /device:TPU:0, one launch (start us, length us, event | category | flops | bytes accessed | tf_op | source)
XLA Modules:
  0.0 263.9 jit_solution(6982499845974031834)
XLA Ops:
  10.8 3.6 %collective-permute-start.1 = (bf16[128,1024]{1,0:T(8,128)(2,1)S(1)}, bf16[128,1024]{1,0:T(8,128)(2,1)S(1)}, u32[]{:S(2)}, u32[]{:S(2)}) collective-permute-start(bf16[128,1024]{1,0:T(8,128)(2,1)S(1)} %get-tuple-element.67), channel_id=1, source_target_pairs={{0,8},{1,9},{2,10},{3,11},{4,12},{5,13},{6,14},{7,15},{8,0},{9,1},... | collective-permute-start | bytes 786440 | tf_op jit(solution)/shard_map/ppermute | solution.py:47
  33.4 7.2 %collective-permute-done.5.p3 = bf16[4,128,1024]{2,1,0:T(8,128)(2,1)S(1)} collective-permute-done((bf16[4,128,1024]{2,1,0:T(8,128)(2,1)S(1)}, bf16[4,128,1024]{2,1,0:T(8,128)(2,1)S(1)}, u32[]{:S(2)}, u32[]{:S(2)}) %collective-permute-start.5) | collective-permute-done | bytes 1048608 | tf_op jit(solution)/shard_map/ppermute | solution.py:47
  44.1 6.0 %shard_map.79 = (bf16[4,128,1024]{2,1,0:T(8,128)(2,1)S(1)}, bf16[4,128,1024]{2,1,0:T(8,128)(2,1)S(1)}, bf16[4,128,1024]{2,1,0:T(8,128)(2,1)S(1)}, bf16[4,128,1024]{2,1,0:T(8,128)(2,1)S(1)}) custom-call(s32[7]{0:T(128)S(1)} %stack.115.ids, bf16[4,128,1024]{2,1,0:T(8,128)(2,1)S(1)} %pad_maximum_fusion.p0, bf16[4,128,1024]{2,1,0:T(8,128)(2,1)S(1)} %collective-permute-done.3.p1, ...), custom_call_target="tpu_custom_call" | custom-call | flops 3221225472 | bytes 8000000 | tf_op jit(solution)/shard_map/pallas_call | solution.py:68
  50.2 3.6 %collective-permute-done.4.low = bf16[2,128,1024]{2,1,0:T(8,128)(2,1)S(1)} collective-permute-done((bf16[2,128,1024]{2,1,0:T(8,128)(2,1)S(1)}, bf16[2,128,1024]{2,1,0:T(8,128)(2,1)S(1)}, u32[]{:S(2)}, u32[]{:S(2)}) %collective-permute-start.4) | collective-permute-done | bytes 524320 | tf_op jit(solution)/shard_map/ppermute | solution.py:47
  56.2 4.1 %collective-permute-start.12 = (bf16[4,128,1024]{2,1,0:T(8,128)(2,1)S(1)}, bf16[4,128,1024]{2,1,0:T(8,128)(2,1)S(1)}, u32[]{:S(2)}, u32[]{:S(2)}) collective-permute-start(bf16[4,128,1024]{2,1,0:T(8,128)(2,1)S(1)} %get-tuple-element.78), channel_id=1, source_target_pairs={{0,12},{1,13},{2,14},{3,15},{4,0},{5,1},{6,2},{7,3},{8,4},{9,5},{1... | collective-permute-start | bytes 3145736 | tf_op jit(solution)/shard_map/ppermute | solution.py:47
  66.2 10.2 %collective-permute-done.15.o1 = bf16[128,1024]{1,0:T(8,128)(2,1)S(1)} collective-permute-done((bf16[128,1024]{1,0:T(8,128)(2,1)S(1)}, bf16[128,1024]{1,0:T(8,128)(2,1)S(1)}, u32[]{:S(2)}, u32[]{:S(2)}) %collective-permute-start.15) | collective-permute-done | bytes 262176 | tf_op jit(solution)/shard_map/ppermute | solution.py:47
  79.0 3.9 %collective-permute-done.17.o3 = bf16[128,1024]{1,0:T(8,128)(2,1)S(1)} collective-permute-done((bf16[128,1024]{1,0:T(8,128)(2,1)S(1)}, bf16[128,1024]{1,0:T(8,128)(2,1)S(1)}, u32[]{:S(2)}, u32[]{:S(2)}) %collective-permute-start.17) | collective-permute-done | bytes 262176 | tf_op jit(solution)/shard_map/ppermute | solution.py:47
  82.9 6.2 %collective-permute-done.12.z1 = bf16[4,128,1024]{2,1,0:T(8,128)(2,1)S(1)} collective-permute-done((bf16[4,128,1024]{2,1,0:T(8,128)(2,1)S(1)}, bf16[4,128,1024]{2,1,0:T(8,128)(2,1)S(1)}, u32[]{:S(2)}, u32[]{:S(2)}) %collective-permute-start.12) | collective-permute-done | bytes 1048608 | tf_op jit(solution)/shard_map/ppermute | solution.py:47
  89.1 3.2 %collective-permute-done.14.z3 = bf16[4,128,1024]{2,1,0:T(8,128)(2,1)S(1)} collective-permute-done((bf16[4,128,1024]{2,1,0:T(8,128)(2,1)S(1)}, bf16[4,128,1024]{2,1,0:T(8,128)(2,1)S(1)}, u32[]{:S(2)}, u32[]{:S(2)}) %collective-permute-start.14) | collective-permute-done | bytes 1048608 | tf_op jit(solution)/shard_map/ppermute | solution.py:47
  104.8 5.0 %collective-permute-done.30 = f32[8,1,1024]{2,1,0:T(1,128)S(1)} collective-permute-done((f32[8,1,1024]{2,1,0:T(1,128)S(1)}, f32[8,1,1024]{2,1,0:T(1,128)S(1)}, u32[]{:S(2)}, u32[]{:S(2)}) %collective-permute-start.30) | collective-permute-done | bytes 32800 | tf_op jit(solution)/shard_map/ppermute | solution.py:47
  115.3 5.4 %shard_map.83 = (bf16[128,1024]{1,0:T(8,128)(2,1)S(1)}, bf16[128,1024]{1,0:T(8,128)(2,1)S(1)}, bf16[128,1024]{1,0:T(8,128)(2,1)S(1)}, bf16[128,1024]{1,0:T(8,128)(2,1)S(1)}, bf16[8,16,4096]{2,1,0:T(8,128)(2,1)S(1)}) custom-call(s32[7]{0:T(128)S(1)} %stack.115.ids, f32[2,8,32]{2,1,0:T(8,128)S(1)} %bitcast.68, ...), custom_call_target="tpu_custom_call" | custom-call | flops 20000000 | bytes 8000000 | tf_op jit(solution)/shard_map/pallas_call | solution.py:68
  124.0 7.2 %collective-permute-done.32 = bf16[128,1024]{1,0:T(8,128)(2,1)S(1)} collective-permute-done((bf16[128,1024]{1,0:T(8,128)(2,1)S(1)}, bf16[128,1024]{1,0:T(8,128)(2,1)S(1)}, u32[]{:S(2)}, u32[]{:S(2)}) %collective-permute-start.32) | collective-permute-done | bytes 262176 | tf_op jit(solution)/shard_map/ppermute | solution.py:47
  134.3 12.8 %collective-permute-done.37.p3 = bf16[4,128,1024]{2,1,0:T(8,128)(2,1)S(1)} collective-permute-done((bf16[4,128,1024]{2,1,0:T(8,128)(2,1)S(1)}, bf16[4,128,1024]{2,1,0:T(8,128)(2,1)S(1)}, u32[]{:S(2)}, u32[]{:S(2)}) %collective-permute-start.37) | collective-permute-done | bytes 1048608 | tf_op jit(solution)/shard_map/ppermute | solution.py:47
  151.9 4.7 %collective-permute-done.38.high = bf16[2,128,1024]{2,1,0:T(8,128)(2,1)S(1)} collective-permute-done((bf16[2,128,1024]{2,1,0:T(8,128)(2,1)S(1)}, bf16[2,128,1024]{2,1,0:T(8,128)(2,1)S(1)}, u32[]{:S(2)}, u32[]{:S(2)}) %collective-permute-start.38) | collective-permute-done | bytes 524320 | tf_op jit(solution)/shard_map/ppermute | solution.py:47
  156.6 3.8 %collective-permute-done.36.low = bf16[2,128,1024]{2,1,0:T(8,128)(2,1)S(1)} collective-permute-done((bf16[2,128,1024]{2,1,0:T(8,128)(2,1)S(1)}, bf16[2,128,1024]{2,1,0:T(8,128)(2,1)S(1)}, u32[]{:S(2)}, u32[]{:S(2)}) %collective-permute-start.36) | collective-permute-done | bytes 524320 | tf_op jit(solution)/shard_map/ppermute | solution.py:47
  160.4 7.9 %shard_map.90 = (bf16[1024,256]{1,0:T(8,128)(2,1)S(1)}, bf16[1024,256]{1,0:T(8,128)(2,1)S(1)}, bf16[1024,256]{1,0:T(8,128)(2,1)S(1)}, bf16[1024,256]{1,0:T(8,128)(2,1)S(1)}) custom-call(s32[7]{0:T(128)S(1)} %stack.115.ids, bf16[1024,2048]{1,0:T(8,128)(2,1)S(1)} %shard_map.89.left, bf16[4,128,1024]{2,1,0:T(8,128)(2,1)S(1)} %pad_maximum_fusion.1.p0, ...), custom_call_target="tpu_custom_call" | custom-call | flops 4294967296 | bytes 8000000 | tf_op jit(solution)/shard_map/pallas_call | solution.py:68
  172.9 6.5 %shard_map.84 = (bf16[4,128,1024]{2,1,0:T(8,128)(2,1)S(1)}, bf16[4,128,1024]{2,1,0:T(8,128)(2,1)S(1)}, bf16[4,128,1024]{2,1,0:T(8,128)(2,1)S(1)}, bf16[4,128,1024]{2,1,0:T(8,128)(2,1)S(1)}) custom-call(s32[7]{0:T(128)S(1)} %stack.115.ids, bf16[4,128,1024]{2,1,0:T(8,128)(2,1)S(1)} %pad_maximum_fusion.1.p0, ...), custom_call_target="tpu_custom_call" | custom-call | flops 3221225472 | bytes 8000000 | tf_op jit(solution)/shard_map/pallas_call | solution.py:68
  188.3 4.3 %collective-permute-done.55.q2 = bf16[1024,256]{1,0:T(8,128)(2,1)S(1)} collective-permute-done((bf16[1024,256]{1,0:T(8,128)(2,1)S(1)}, bf16[1024,256]{1,0:T(8,128)(2,1)S(1)}, u32[]{:S(2)}, u32[]{:S(2)}) %collective-permute-start.55) | collective-permute-done | bytes 524320 | tf_op jit(solution)/shard_map/ppermute | solution.py:51
  194.6 8.4 %collective-permute-done.42.o1 = bf16[128,1024]{1,0:T(8,128)(2,1)S(1)} collective-permute-done((bf16[128,1024]{1,0:T(8,128)(2,1)S(1)}, bf16[128,1024]{1,0:T(8,128)(2,1)S(1)}, u32[]{:S(2)}, u32[]{:S(2)}) %collective-permute-start.42) | collective-permute-done | bytes 262176 | tf_op jit(solution)/shard_map/ppermute | solution.py:47
  203.0 21.0 %collective-permute-done.57.r1 = bf16[256,256]{1,0:T(8,128)(2,1)S(1)} collective-permute-done((bf16[256,256]{1,0:T(8,128)(2,1)S(1)}, bf16[256,256]{1,0:T(8,128)(2,1)S(1)}, u32[]{:S(2)}, u32[]{:S(2)}) %collective-permute-start.57) | collective-permute-done | bytes 131104 | tf_op jit(solution)/shard_map/ppermute | solution.py:51
  224.1 5.0 %collective-permute-done.59.r3 = bf16[256,256]{1,0:T(8,128)(2,1)S(1)} collective-permute-done((bf16[256,256]{1,0:T(8,128)(2,1)S(1)}, bf16[256,256]{1,0:T(8,128)(2,1)S(1)}, u32[]{:S(2)}, u32[]{:S(2)}) %collective-permute-start.59) | collective-permute-done | bytes 131104 | tf_op jit(solution)/shard_map/ppermute | solution.py:51
  229.7 2.9 %collective-permute-done.43.o2 = bf16[128,1024]{1,0:T(8,128)(2,1)S(1)} collective-permute-done((bf16[128,1024]{1,0:T(8,128)(2,1)S(1)}, bf16[128,1024]{1,0:T(8,128)(2,1)S(1)}, u32[]{:S(2)}, u32[]{:S(2)}) %collective-permute-start.43) | collective-permute-done | bytes 262176 | tf_op jit(solution)/shard_map/ppermute | solution.py:47
  249.6 5.8 %collective-permute-done.53 = f32[8,1,1024]{2,1,0:T(1,128)S(1)} collective-permute-done((f32[8,1,1024]{2,1,0:T(1,128)S(1)}, f32[8,1,1024]{2,1,0:T(1,128)S(1)}, u32[]{:S(2)}, u32[]{:S(2)}) %collective-permute-start.53) | collective-permute-done | bytes 32800 | tf_op jit(solution)/shard_map/ppermute | solution.py:47
  259.5 4.4 %shard_map.88 = (bf16[8,16,4096]{2,1,0:T(8,128)(2,1)}, bf16[8,16,4096]{2,1,0:T(8,128)(2,1)}) custom-call(s32[7]{0:T(128)S(1)} %stack.115.ids, f32[2,8,32]{2,1,0:T(8,128)S(1)} %bitcast.70, bf16[128,1024]{1,0:T(8,128)(2,1)S(1)} %get-tuple-element.107.r0, bf16[128,1024]{1,0:T(8,128)(2,1)S(1)} %collective-permute-done.45.r1, ...), custom_call_target="tpu_custom_call" | custom-call | flops 20000000 | bytes 8000000 | tf_op jit(solution)/shard_map/pallas_call | solution.py:68
  (155 shorter events, 109.7 us)
Async XLA Ops:
  17.7 12.1 %collective-permute-start.8 = (bf16[128,1024]{1,0:T(8,128)(2,1)S(1)}, bf16[128,1024]{1,0:T(8,128)(2,1)S(1)}, u32[]{:S(2)}, u32[]{:S(2)}) collective-permute-start(bf16[128,1024]{1,0:T(8,128)(2,1)S(1)} %get-tuple-element.71), channel_id=1, source_target_pairs={{0,2},{1,3},{2,0},{3,1},{4,6},{5,7},{6,4},{7,5},{8,10},{9,11},{10,... | collective-permute-start | bytes 786440 | tf_op jit(solution)/shard_map/ppermute | solution.py:51
  22.1 18.4 %collective-permute-start.5 = (bf16[4,128,1024]{2,1,0:T(8,128)(2,1)S(1)}, bf16[4,128,1024]{2,1,0:T(8,128)(2,1)S(1)}, u32[]{:S(2)}, u32[]{:S(2)}) collective-permute-start(bf16[4,128,1024]{2,1,0:T(8,128)(2,1)S(1)} %pad_maximum_fusion.p0), channel_id=1, source_target_pairs={{0,3},{1,0},{2,1},{3,2},{4,7},{5,4},{6,5},{7,6},{8,11},{9,8},{10,9... | collective-permute-start | bytes 3145736 | tf_op jit(solution)/shard_map/ppermute | solution.py:47
  24.8 18.5 %collective-permute-start.3 = (bf16[4,128,1024]{2,1,0:T(8,128)(2,1)S(1)}, bf16[4,128,1024]{2,1,0:T(8,128)(2,1)S(1)}, u32[]{:S(2)}, u32[]{:S(2)}) collective-permute-start(bf16[4,128,1024]{2,1,0:T(8,128)(2,1)S(1)} %pad_maximum_fusion.p0), channel_id=1, source_target_pairs={{0,1},{1,2},{2,3},{3,0},{4,5},{5,6},{6,7},{7,4},{8,9},{9,10},{10,1... | collective-permute-start | bytes 3145736 | tf_op jit(solution)/shard_map/ppermute | solution.py:47
  29.9 13.5 %collective-permute-start.10 = (bf16[4,64,1024]{2,1,0:T(8,128)(2,1)S(1)}, bf16[4,64,1024]{2,1,0:T(8,128)(2,1)S(1)}, u32[]{:S(2)}, u32[]{:S(2)}) collective-permute-start(bf16[4,64,1024]{2,1,0:T(8,128)(2,1)S(1)} %pad_maximum_fusion.2.a0), channel_id=1, source_target_pairs={{0,32},{32,64},{64,96},{96,0},{1,33},{33,65},{65,97},{97,1},{2,34}... | collective-permute-start | bytes 1572872 | tf_op jit(solution)/shard_map/ppermute | solution.py:51
  56.2 32.9 %collective-permute-start.12 = (bf16[4,128,1024]{2,1,0:T(8,128)(2,1)S(1)}, bf16[4,128,1024]{2,1,0:T(8,128)(2,1)S(1)}, u32[]{:S(2)}, u32[]{:S(2)}) collective-permute-start(bf16[4,128,1024]{2,1,0:T(8,128)(2,1)S(1)} %get-tuple-element.78), channel_id=1, source_target_pairs={{0,12},{1,13},{2,14},{3,15},{4,0},{5,1},{6,2},{7,3},{8,4},{9,5},{1... | collective-permute-start | bytes 3145736 | tf_op jit(solution)/shard_map/ppermute | solution.py:47
  60.3 28.8 %collective-permute-start.13 = (bf16[4,128,1024]{2,1,0:T(8,128)(2,1)S(1)}, bf16[4,128,1024]{2,1,0:T(8,128)(2,1)S(1)}, u32[]{:S(2)}, u32[]{:S(2)}) collective-permute-start(bf16[4,128,1024]{2,1,0:T(8,128)(2,1)S(1)} %get-tuple-element.79), channel_id=1, source_target_pairs={{0,8},{1,9},{2,10},{3,11},{4,12},{5,13},{6,14},{7,15},{8,0},{9,1},... | collective-permute-start | bytes 3145736 | tf_op jit(solution)/shard_map/ppermute | solution.py:47
  60.3 32.0 %collective-permute-start.14 = (bf16[4,128,1024]{2,1,0:T(8,128)(2,1)S(1)}, bf16[4,128,1024]{2,1,0:T(8,128)(2,1)S(1)}, u32[]{:S(2)}, u32[]{:S(2)}) collective-permute-start(bf16[4,128,1024]{2,1,0:T(8,128)(2,1)S(1)} %get-tuple-element.80), channel_id=1, source_target_pairs={{0,4},{1,5},{2,6},{3,7},{4,8},{5,9},{6,10},{7,11},{8,12},{9,13},{1... | collective-permute-start | bytes 3145736 | tf_op jit(solution)/shard_map/ppermute | solution.py:47
  64.4 12.0 %collective-permute-start.15 = (bf16[128,1024]{1,0:T(8,128)(2,1)S(1)}, bf16[128,1024]{1,0:T(8,128)(2,1)S(1)}, u32[]{:S(2)}, u32[]{:S(2)}) collective-permute-start(bf16[128,1024]{1,0:T(8,128)(2,1)S(1)} %get-tuple-element.82), channel_id=1, source_target_pairs={{0,1},{1,2},{2,3},{3,0},{4,5},{5,6},{6,7},{7,4},{8,9},{9,10},{10,1... | collective-permute-start | bytes 786440 | tf_op jit(solution)/shard_map/ppermute | solution.py:47
  64.5 14.5 %collective-permute-start.16 = (bf16[128,1024]{1,0:T(8,128)(2,1)S(1)}, bf16[128,1024]{1,0:T(8,128)(2,1)S(1)}, u32[]{:S(2)}, u32[]{:S(2)}) collective-permute-start(bf16[128,1024]{1,0:T(8,128)(2,1)S(1)} %get-tuple-element.83), channel_id=1, source_target_pairs={{0,2},{1,3},{2,0},{3,1},{4,6},{5,7},{6,4},{7,5},{8,10},{9,11},{10,... | collective-permute-start | bytes 786440 | tf_op jit(solution)/shard_map/ppermute | solution.py:47
  97.1 13.1 %collective-permute-start.18 = (bf16[128,1024]{1,0:T(8,128)(2,1)S(1)}, bf16[128,1024]{1,0:T(8,128)(2,1)S(1)}, u32[]{:S(2)}, u32[]{:S(2)}) collective-permute-start(bf16[128,1024]{1,0:T(8,128)(2,1)S(1)} %get-tuple-element.86), channel_id=1, source_target_pairs={{0,3},{1,0},{2,1},{3,2},{4,7},{5,4},{6,5},{7,6},{8,11},{9,8},{10,9... | collective-permute-start | bytes 786440 | tf_op jit(solution)/shard_map/ppermute | solution.py:47
  97.6 13.1 %collective-permute-start.19 = (bf16[128,1024]{1,0:T(8,128)(2,1)S(1)}, bf16[128,1024]{1,0:T(8,128)(2,1)S(1)}, u32[]{:S(2)}, u32[]{:S(2)}) collective-permute-start(bf16[128,1024]{1,0:T(8,128)(2,1)S(1)} %get-tuple-element.87), channel_id=1, source_target_pairs={{0,2},{1,3},{2,0},{3,1},{4,6},{5,7},{6,4},{7,5},{8,10},{9,11},{10,... | collective-permute-start | bytes 786440 | tf_op jit(solution)/shard_map/ppermute | solution.py:47
  132.2 14.9 %collective-permute-start.37 = (bf16[4,128,1024]{2,1,0:T(8,128)(2,1)S(1)}, bf16[4,128,1024]{2,1,0:T(8,128)(2,1)S(1)}, u32[]{:S(2)}, u32[]{:S(2)}) collective-permute-start(bf16[4,128,1024]{2,1,0:T(8,128)(2,1)S(1)} %pad_maximum_fusion.1.p0), channel_id=1, source_target_pairs={{0,12},{1,13},{2,14},{3,15},{4,0},{5,1},{6,2},{7,3},{8,4},{9,5},{1... | collective-permute-start | bytes 3145736 | tf_op jit(solution)/shard_map/ppermute | solution.py:47
  133.8 16.1 %collective-permute-start.35 = (bf16[4,128,1024]{2,1,0:T(8,128)(2,1)S(1)}, bf16[4,128,1024]{2,1,0:T(8,128)(2,1)S(1)}, u32[]{:S(2)}, u32[]{:S(2)}) collective-permute-start(bf16[4,128,1024]{2,1,0:T(8,128)(2,1)S(1)} %pad_maximum_fusion.1.p0), channel_id=1, source_target_pairs={{0,4},{1,5},{2,6},{3,7},{4,8},{5,9},{6,10},{7,11},{8,12},{9,13},{1... | collective-permute-start | bytes 3145736 | tf_op jit(solution)/shard_map/ppermute | solution.py:47
  168.4 17.2 %collective-permute-start.54 = (bf16[1024,256]{1,0:T(8,128)(2,1)S(1)}, bf16[1024,256]{1,0:T(8,128)(2,1)S(1)}, u32[]{:S(2)}, u32[]{:S(2)}) collective-permute-start(bf16[1024,256]{1,0:T(8,128)(2,1)S(1)} %get-tuple-element.116), channel_id=1, source_target_pairs={{0,32},{32,64},{64,96},{96,0},{1,33},{33,65},{65,97},{97,1},{2,34}... | collective-permute-start | bytes 1572872 | tf_op jit(solution)/shard_map/ppermute | solution.py:51
  169.9 22.7 %collective-permute-start.55 = (bf16[1024,256]{1,0:T(8,128)(2,1)S(1)}, bf16[1024,256]{1,0:T(8,128)(2,1)S(1)}, u32[]{:S(2)}, u32[]{:S(2)}) collective-permute-start(bf16[1024,256]{1,0:T(8,128)(2,1)S(1)} %get-tuple-element.117), channel_id=1, source_target_pairs={{0,64},{32,96},{64,0},{96,32},{1,65},{33,97},{65,1},{97,33},{2,66}... | collective-permute-start | bytes 1572872 | tf_op jit(solution)/shard_map/ppermute | solution.py:51
  179.4 14.4 %collective-permute-start.56 = (bf16[1024,256]{1,0:T(8,128)(2,1)S(1)}, bf16[1024,256]{1,0:T(8,128)(2,1)S(1)}, u32[]{:S(2)}, u32[]{:S(2)}) collective-permute-start(bf16[1024,256]{1,0:T(8,128)(2,1)S(1)} %get-tuple-element.118), channel_id=1, source_target_pairs={{0,96},{32,0},{64,32},{96,64},{1,97},{33,1},{65,33},{97,65},{2,98}... | collective-permute-start | bytes 1572872 | tf_op jit(solution)/shard_map/ppermute | solution.py:51
  182.9 52.5 %collective-permute-start.39 = (bf16[4,128,1024]{2,1,0:T(8,128)(2,1)S(1)}, bf16[4,128,1024]{2,1,0:T(8,128)(2,1)S(1)}, u32[]{:S(2)}, u32[]{:S(2)}) collective-permute-start(bf16[4,128,1024]{2,1,0:T(8,128)(2,1)S(1)} %get-tuple-element.99), channel_id=1, source_target_pairs={{0,3},{1,0},{2,1},{3,2},{4,7},{5,4},{6,5},{7,6},{8,11},{9,8},{10,9... | collective-permute-start | bytes 3145736 | tf_op jit(solution)/shard_map/ppermute | solution.py:47
  185.6 49.8 %collective-permute-start.40 = (bf16[4,128,1024]{2,1,0:T(8,128)(2,1)S(1)}, bf16[4,128,1024]{2,1,0:T(8,128)(2,1)S(1)}, u32[]{:S(2)}, u32[]{:S(2)}) collective-permute-start(bf16[4,128,1024]{2,1,0:T(8,128)(2,1)S(1)} %get-tuple-element.100), channel_id=1, source_target_pairs={{0,2},{1,3},{2,0},{3,1},{4,6},{5,7},{6,4},{7,5},{8,10},{9,11},{10,... | collective-permute-start | bytes 3145736 | tf_op jit(solution)/shard_map/ppermute | solution.py:47
  185.6 49.8 %collective-permute-start.41 = (bf16[4,128,1024]{2,1,0:T(8,128)(2,1)S(1)}, bf16[4,128,1024]{2,1,0:T(8,128)(2,1)S(1)}, u32[]{:S(2)}, u32[]{:S(2)}) collective-permute-start(bf16[4,128,1024]{2,1,0:T(8,128)(2,1)S(1)} %get-tuple-element.101), channel_id=1, source_target_pairs={{0,1},{1,2},{2,3},{3,0},{4,5},{5,6},{6,7},{7,4},{8,9},{9,10},{10,1... | collective-permute-start | bytes 3145736 | tf_op jit(solution)/shard_map/ppermute | solution.py:47
  194.6 29.5 %collective-permute-start.57 = (bf16[256,256]{1,0:T(8,128)(2,1)S(1)}, bf16[256,256]{1,0:T(8,128)(2,1)S(1)}, u32[]{:S(2)}, u32[]{:S(2)}) collective-permute-start(bf16[256,256]{1,0:T(8,128)(2,1)S(1)} %get-tuple-element.120), channel_id=1, source_target_pairs={{0,1},{1,2},{2,3},{3,0},{4,5},{5,6},{6,7},{7,4},{8,9},{9,10},{10,1... | collective-permute-start | bytes 393224 | tf_op jit(solution)/shard_map/ppermute | solution.py:51
  203.0 21.0 %collective-permute-start.58 = (bf16[256,256]{1,0:T(8,128)(2,1)S(1)}, bf16[256,256]{1,0:T(8,128)(2,1)S(1)}, u32[]{:S(2)}, u32[]{:S(2)}) collective-permute-start(bf16[256,256]{1,0:T(8,128)(2,1)S(1)} %get-tuple-element.121), channel_id=1, source_target_pairs={{0,2},{1,3},{2,0},{3,1},{4,6},{5,7},{6,4},{7,5},{8,10},{9,11},{10,... | collective-permute-start | bytes 393224 | tf_op jit(solution)/shard_map/ppermute | solution.py:51
  243.2 16.3 %collective-permute-start.45 = (bf16[128,1024]{1,0:T(8,128)(2,1)S(1)}, bf16[128,1024]{1,0:T(8,128)(2,1)S(1)}, u32[]{:S(2)}, u32[]{:S(2)}) collective-permute-start(bf16[128,1024]{1,0:T(8,128)(2,1)S(1)} %get-tuple-element.108), channel_id=1, source_target_pairs={{0,12},{1,13},{2,14},{3,15},{4,0},{5,1},{6,2},{7,3},{8,4},{9,5},{1... | collective-permute-start | bytes 786440 | tf_op jit(solution)/shard_map/ppermute | solution.py:47
  244.4 15.1 %collective-permute-start.46 = (bf16[128,1024]{1,0:T(8,128)(2,1)S(1)}, bf16[128,1024]{1,0:T(8,128)(2,1)S(1)}, u32[]{:S(2)}, u32[]{:S(2)}) collective-permute-start(bf16[128,1024]{1,0:T(8,128)(2,1)S(1)} %get-tuple-element.109), channel_id=1, source_target_pairs={{0,8},{1,9},{2,10},{3,11},{4,12},{5,13},{6,14},{7,15},{8,0},{9,1},... | collective-permute-start | bytes 786440 | tf_op jit(solution)/shard_map/ppermute | solution.py:47
  244.8 14.7 %collective-permute-start.47 = (bf16[128,1024]{1,0:T(8,128)(2,1)S(1)}, bf16[128,1024]{1,0:T(8,128)(2,1)S(1)}, u32[]{:S(2)}, u32[]{:S(2)}) collective-permute-start(bf16[128,1024]{1,0:T(8,128)(2,1)S(1)} %get-tuple-element.110), channel_id=1, source_target_pairs={{0,4},{1,5},{2,6},{3,7},{4,8},{5,9},{6,10},{7,11},{8,12},{9,13},{1... | collective-permute-start | bytes 786440 | tf_op jit(solution)/shard_map/ppermute | solution.py:47
  (48 other events, 396.0 us)
where the time goes:
time: 265 us; the launch traced here: 264 us
  waiting for transfers between devices  136 us (51%)
  starting transfers between devices  67.1 us (25%)
  Pallas kernels  52.9 us (20%)
  local copies, waits for them, and re-layouts  5.66 us (2%)
    ppermute x44, waiting for transfers between devices, shift(): return lax.ppermute(value, CHIP, pairs)  99.8 us
    pallas_call x18, Pallas kernels, call(): pl.pallas_call(body, grid_spec=pltpu.PrefetchScalarGridSpec(num_scalar_pr...  52.9 us
    ppermute x44, starting transfers between devices, shift(): return lax.ppermute(value, CHIP, pairs)  47 us
    ppermute x14, waiting for transfers between devices, ring(): lax.ppermute(value, axis, [(i, (i + steps) % SIDE) for i in range(SIDE)])  35.3 us
    ppermute x14, starting transfers between devices, ring(): lax.ppermute(value, axis, [(i, (i + steps) % SIDE) for i in range(SIDE)])  19.1 us
    unnamed x18, local copies, waits for them, and re-layouts  5.36 us
  transfers between devices with their start and end apart: 63, of which 28 were waited for; matrix products, arithmetic and copies ran while one was open for 0% of the time, Pallas kernels for 11%

commit v1 on v0

--- a/solution.py
+++ b/solution.py
@@ -13,6 +13,8 @@
 CHIP = ("section", "tensor_0", "tensor_1")
 DP_TENSOR = ("dp", "tensor_0", "tensor_1")
 SIDE = 4
+ROWS, COLUMNS = "rows", "columns"
+DP, SECTION, FAST = "dp", "section", "tensor_1"
 BLOCK = 128
 PER = 8
 STEPS = 2
@@ -27,7 +29,7 @@
 
 
 def on_z(s, phase, along):
-    return ((s + phase) % 2 == 0) == (along == "rows")
+    return ((s + phase) % 2 == 0) == (along == ROWS)
 
 
 def position(s, z, y):
@@ -52,7 +54,7 @@
 
 
 def crossed_over(value):
-    return lax.ppermute(value, "section", [(0, 1), (1, 0)])
+    return lax.ppermute(value, SECTION, [(0, 1), (1, 0)])
 
 
 def lanes(block):
@@ -145,14 +147,17 @@
         def step(m):
             i = start + m
             at_rows = pl.ds(pl.multiple_of(m * rows, rows), rows)
-            for j in range(SIDE):
-                for inner in range(PER):
+
+            def sweep(inner):
+                for j in range(SIDE):
                     at = column(ids[2], j, inner)
                     hidden = f32(near[0, m, :, at]) * scale_at(
                         scales, 0, i, ids[2], j, inner
                     ) + f32(arriving[m, :, at])
                     behind = f32(far[0, m, :, at]) * scale_at(scales, 1, i, ids[2], j, inner)
-                    offsets[j][at_rows, lanes(inner)] = (hidden - behind).astype(jnp.bfloat16)
+                    offsets[j][at_rows, tile(inner, BLOCK)] = (hidden - behind).astype(jnp.bfloat16)
+
+            each_micro(PER, sweep)
 
         each_micro(count, step)
 
@@ -184,37 +189,50 @@
         each_micro(SIDE, step)
 
 
-def early_body(phase, ids, p0, p1, p3, matrix, *outs):
-    for j, group in ((0, p0), (1, p1), (3, p3)):
-        def read(group=group):
-            return group[...].reshape(-1, group.shape[-1])
-
-        def store(product, cols, j=j):
+def both(low, high):
+    return jnp.concatenate([low[0], low[1], high[0], high[1]], axis=0)
+
+
+def early_body(phase, ids, *refs):
+    groups, matrix = refs[:6], refs[6]
+    lows, highs = refs[7 : 7 + SIDE], refs[7 + SIDE :]
+    for at, (outs, row) in enumerate(((lows, 0), (lows, 1), (highs, 1))):
+        def store(product, cols, outs=outs, row=row):
             count = product.shape[0] // SIDE
             for k in range(SIDE):
-                outs[k][j, :, cols] = product[k * count : (k + 1) * count].astype(jnp.bfloat16)
-
-        multiply(phase, ids, read, matrix, store)
+                outs[k][row, :, cols] = product[k * count : (k + 1) * count].astype(jnp.bfloat16)
+
+        multiply(
+            phase, ids, functools.partial(both, *groups[2 * at : 2 * at + 2]), matrix, store
+        )
 
 
 def late_body(phase, ids, low, high, matrix, *refs):
     outs = refs[SIDE:]
-
-    def read():
-        return jnp.concatenate([low[0], low[1], high[0], high[1]], axis=0)
 
     def store(product, cols):
         count = product.shape[0] // SIDE
         for k in range(SIDE):
             outs[k][0, :, cols] = product[k * count : (k + 1) * count].astype(jnp.bfloat16)
 
-    multiply(phase, ids, read, matrix, store)
-
-
-def combine_body(phase, ids, z0, z1, z2, z3, o0, o1, o2, o3, v0, v1, v2, v3, peak):
+    multiply(phase, ids, functools.partial(both, low, high), matrix, store)
+
+
+def add_body(ids, a0, a1, b0, b1, a_out, b_out):
+    rows = a0.shape[1] // SIDE
+
+    def step(t):
+        at = (t // SIDE, tile(lax.rem(t, SIDE), rows), slice(None))
+        a_out[at] = (f32(a0[at]) + f32(a1[at])).astype(jnp.bfloat16)
+        b_out[at] = (f32(b0[at]) + f32(b1[at])).astype(jnp.bfloat16)
+
+    each_micro(2 * SIDE, step)
+
+
+def combine_body(phase, ids, l0, l1, l3, h0, h1, h3, o0, o1, o2, o3, v0, v1, v2, v3, peak):
     offsets, outs = (o0, o1, o2, o3), (v0, v1, v2, v3)
     count = peak.shape[0]
-    rows = z0.shape[1] // count
+    rows = l0.shape[1] // count
     forward = ids[0] == phase
 
     def step(m):
@@ -223,9 +241,8 @@
             cols = lanes(inner)
             best = jnp.zeros((rows, BLOCK), jnp.float32)
             for j in range(SIDE):
-                value = (f32(z0[j, at, cols]) + f32(z1[j, at, cols])) + (
-                    f32(z2[j, at, cols]) + f32(z3[j, at, cols])
-                )
+                terms = (l0, l1, l3) if j < 2 else (h0, h1, h3)
+                value = sum(f32(term[j % 2, at, cols]) for term in terms)
                 value = value + jnp.where(forward, f32(offsets[j][at, cols]), 0.0)
                 outs[j][at, cols] = value.astype(jnp.bfloat16)
                 best = jnp.maximum(best, jnp.abs(value))
@@ -261,11 +278,14 @@
         at_rows = pl.ds(pl.multiple_of(m * rows, rows), rows)
 
         def load(deltas, peaks, place):
-            for j in range(SIDE):
-                for inner in range(PER):
+            def sweep(inner):
+                cols = tile(inner, BLOCK)
+                for j in range(SIDE):
                     sent[m, :, column(place, j, inner)] = softened(
-                        f32(deltas[j][at_rows, lanes(inner)]), peaks[j, i, :, lanes(inner)]
+                        f32(deltas[j][at_rows, cols]), peaks[j, i, :, cols]
                     )
+
+            each_micro(PER, sweep)
 
         def read(block, slot):
             at = lanes(block)
@@ -354,13 +374,16 @@
                 at = lanes(block)
                 back = f32(cot[m, :, at]) + inverse * (raw[:, at] - hidden[:, at] * mean)
                 grads[m, :, at] = back.astype(jnp.bfloat16)
-            for j in range(SIDE):
-                for inner in range(PER):
+
+            def sweep(inner):
+                for j in range(SIDE):
                     at = column(ids[4], j, inner)
                     behind = f32(far[0, m, :, at]) * scale_at(scales, 1, i, ids[4], j, inner)
-                    offsets[j][at_rows, lanes(inner)] = (hidden[:, at] - behind).astype(
+                    offsets[j][at_rows, tile(inner, BLOCK)] = (hidden[:, at] - behind).astype(
                         jnp.bfloat16
                     )
+
+            each_micro(PER, sweep)
 
         each_micro(count, step)
 
@@ -403,39 +426,42 @@
     def _():
         def step(m):
             at_rows = pl.ds(pl.multiple_of(m * rows, rows), rows)
-            for j in range(SIDE):
-                for inner in range(PER):
+
+            def sweep(inner):
+                for j in range(SIDE):
                     outs[m, :, column(b, j, inner)] = softened(
-                        f32(result[j][at_rows, lanes(inner)]),
-                        peaks[j, start + m, :, lanes(inner)],
+                        f32(result[j][at_rows, tile(inner, BLOCK)]),
+                        peaks[j, start + m, :, tile(inner, BLOCK)],
                     )
+
+            each_micro(PER, sweep)
 
         each_micro(count, step)
         grads[...] = upstream[...]
 
 
-def turn_body(ids, p0, p1, low, high, p3, out):
-    rows = p0.shape[1]
-    for i in range(SIDE):
+def turn_body(ids, *refs):
+    groups, out = refs[: 2 * SIDE], refs[-1]
+    rows = groups[0].shape[1]
+    for half in range(2):
         for j in range(SIDE):
-            if j == 2:
-                source = low[i] if i < 2 else high[i - 2]
-            else:
-                source = (p0, p1, None, p3)[j][i]
-            at = (i * SIDE + j) * rows
-            out[:, at : at + rows] = source.T
-
-
-def gradient_body(ids, left, p0, p1, low, high, p3, *outs):
+            def step(i):
+                out[:, tile((2 * half + i) * SIDE + j, rows)] = groups[2 * j + half][i].T
+
+            each_micro(2, step)
+
+
+def gradient_body(ids, left, *refs):
+    groups, outs, result = refs[: 2 * SIDE], refs[2 * SIDE : -1], refs[-1]
     span = left.shape[0]
     part = span // SIDE
     depth = left.shape[1] // SIDE
 
     def product(rows, columns):
         total = None
-        for i, groups in enumerate(((p0,), (p1,), (low, high), (p3,))):
+        for i in range(SIDE):
             right = jnp.concatenate(
-                [group[j, :, columns] for group in groups for j in range(group.shape[0])], axis=0
+                [groups[2 * i + j // 2][j % 2, :, columns] for j in range(SIDE)], axis=0
             )
             term = jnp.dot(
                 left[rows, i * depth : (i + 1) * depth], right, preferred_element_type=jnp.float32
@@ -443,22 +469,28 @@
             total = term if total is None else total + term
         return total.astype(jnp.bfloat16)
 
+    def places(t):
+        k, n = t // SIDE, lax.rem(t, SIDE)
+        return k, tile(n, part), tile(lax.rem(ids[5] + k, SIDE), part)
+
+    @pl.when(ids[0] == 0)
+    def _():
+        def step(t):
+            k, each, mine = places(t)
+            result[k, each, :] = product(each, mine)
+
+        each_micro(SIDE * SIDE, step)
+
+    @pl.when(ids[0] != 0)
+    def _():
+        def step(t):
+            k, each, mine = places(t)
+            result[k, each, :] = product(mine, each).T
+
+        each_micro(SIDE * SIDE, step)
+
     for k in range(SIDE):
-        mine = tile(lax.rem(ids[5] + k, SIDE), part)
-
-        @pl.when(ids[0] == 0)
-        def _():
-            def step(n):
-                outs[k][tile(n, part), :] = product(tile(n, part), mine)
-
-            each_micro(SIDE, step)
-
-        @pl.when(ids[0] != 0)
-        def _():
-            def step(n):
-                outs[k][tile(n, part), :] = product(mine, tile(n, part)).T
-
-            each_micro(SIDE, step)
+        outs[k][...] = result[k]
 
 
 def total_body(ids, q0, q1, q2, q3, *outs):
@@ -500,10 +532,10 @@
 
 
 def local(in_delta, weight, cache_codes, cache_scales, cotangent):
-    s = lax.axis_index("section")
+    s = lax.axis_index(SECTION)
     z = lax.axis_index("tensor_0")
-    y = lax.axis_index("tensor_1")
-    x = lax.axis_index("dp")
+    y = lax.axis_index(FAST)
+    x = lax.axis_index(DP)
     micro_count, local_rows, width = in_delta.shape
     span = width // SIDE
     bf16, single = jnp.bfloat16, jnp.float32
@@ -523,11 +555,10 @@
     work = [pltpu.VMEM((local_rows, width), single)]
     peak_shape = (micro_count, 1, span)
     peaks_spec = pl.BlockSpec((SIDE, *peak_shape), lambda i, ids: (0, 0, 0, 0))
-    everything = pl.BlockSpec((SIDE, rows, span), lambda i, ids: (0, 0, 0))
     half = pl.BlockSpec((2, rows, span), lambda i, ids: (0, 0, 0))
     full_piece = pl.BlockSpec((rows, span), lambda i, ids: (0, 0))
     square = pl.BlockSpec((span, span), lambda i, ids: (0, 0))
-    cut_shape = jax.ShapeDtypeStruct((SIDE, rows, span), bf16)
+    half_shape = jax.ShapeDtypeStruct((2, rows, span), bf16)
     codes, scales = cache_codes[0], cache_scales[0, :, :, 0, :]
     near = pl.BlockSpec((1, *flat), lambda i, ids: (0, i, 0, 0))
     far = pl.BlockSpec((1, *flat), lambda i, ids: (1, i, 0, 0))
@@ -549,54 +580,76 @@
         [jax.ShapeDtypeStruct((depth, span), bf16)] * SIDE,
         [pl.BlockSpec((depth, span), lambda i, ids: (0, 0))] * SIDE,
     )
-    halves = [halves[0]] + [ring(halves[k], "tensor_1", k) for k in (1, 2, 3)]
+    halves = [halves[0]] + [ring(halves[k], FAST, k) for k in (1, 2, 3)]
     upper = jnp.stack([part[: depth // 2] for part in halves])
     lower = jnp.stack([part[depth // 2 :] for part in halves])
     block = call(
         assemble_body,
         ids,
         (1,),
-        [upper, lower, ring(upper, "dp", 1), ring(lower, "dp", -1)],
+        [upper, lower, ring(upper, DP, 1), ring(lower, DP, -1)],
         [pl.BlockSpec((SIDE, depth // 2, span), lambda i, ids: (0, 0, 0))] * SIDE,
         jax.ShapeDtypeStruct((span, span), bf16),
         square,
     )
 
     def spread_out(pieces, phase):
-        mine = jnp.stack([pieces[0]] + [shift(pieces[k], phase, "rows", k) for k in (1, 2, 3)])
-        after = shift(mine, phase, "columns", 1)
-        before = shift(mine, phase, "columns", -1)
-        low = shift(after[:2], phase, "columns", 1)
-        high = shift(before[2:], phase, "columns", -1)
-        return [mine, after, low, high, before]
+        arrived = [pieces[0]] + [shift(pieces[k], phase, ROWS, k) for k in (1, 2, 3)]
+        low, high = jnp.stack(arrived[:2]), jnp.stack(arrived[2:])
+        after = [shift(low, phase, COLUMNS, 1)]
+        before = [shift(high, phase, COLUMNS, -1)]
+        after.append(shift(high, phase, COLUMNS, 1))
+        before.insert(0, shift(low, phase, COLUMNS, -1))
+        across = [shift(after[0], phase, COLUMNS, 1), shift(before[1], phase, COLUMNS, -1)]
+        return [low, high, *after, *across, *before]
 
     def moved(offsets, phase):
-        return [offsets[0]] + [shift(offsets[j], phase, "columns", j) for j in (1, 2, 3)]
+        return [offsets[0]] + [shift(offsets[j], phase, COLUMNS, j) for j in (1, 2, 3)]
 
     def products(groups, phase):
         made = call(
             functools.partial(early_body, phase),
             ids,
             (1,),
-            [groups[0], groups[1], groups[4], block],
-            [everything] * 3 + [square],
-            [cut_shape] * SIDE,
-            [everything] * SIDE,
+            [*groups[:4], *groups[6:], block],
+            [half] * 6 + [square],
+            [half_shape] * (2 * SIDE),
+            [half] * (2 * SIDE),
             flops=6 * SIDE * rows * span * span,
         )
-        late = pl.BlockSpec((1, rows, span), lambda i, ids: (2, 0, 0))
-        made = call(
+        lows, highs = made[:SIDE], made[SIDE:]
+
+        def sent(value, steps):
+            return shift(value, phase, ROWS, steps)
+
+        opposite_low = sent(lows[2], -1)
+        last_low = sent(lows[3], 1)
+        late = pl.BlockSpec((1, rows, span), lambda i, ids: (0, 0, 0))
+        highs = call(
             functools.partial(late_body, phase),
             ids,
             (1,),
-            [groups[2], groups[3], block, *made],
+            [*groups[4:6], block, *highs],
             [half, half, square] + [pl.BlockSpec(memory_space=pl.ANY)] * SIDE,
-            [cut_shape] * SIDE,
+            [half_shape] * SIDE,
             [late] * SIDE,
             flops=2 * SIDE * rows * span * span,
             aliases={4 + k: k for k in range(SIDE)},
         )
-        return [made[0]] + [shift(made[k], phase, "rows", -k) for k in (1, 2, 3)]
+        opposite_high = sent(highs[2], 1)
+        first_high = sent(highs[1], -1)
+        first_low, last_high = call(
+            add_body,
+            ids,
+            (1,),
+            [lows[1], opposite_low, highs[3], opposite_high],
+            [half] * 4,
+            [half_shape] * 2,
+            [half] * 2,
+        )
+        first_low = sent(first_low, -1)
+        last_high = sent(last_high, 1)
+        return [lows[0], first_low, last_low, highs[0], first_high, last_high]
 
     def returned(arrived, offsets, phase):
         *sent, peak = call(
@@ -604,14 +657,14 @@
             ids,
             (1,),
             [*arrived, *offsets],
-            [everything] * SIDE + [full_piece] * SIDE,
+            [half] * 6 + [full_piece] * SIDE,
             [piece_shape] * SIDE + [jax.ShapeDtypeStruct(peak_shape, single)],
             [full_piece] * SIDE + [pl.BlockSpec(peak_shape, lambda i, ids: (0, 0, 0))],
         )
-        for k, other in [(k, shift(peak, phase, "rows", k)) for k in (1, 2, 3)]:
+        for k, other in [(k, shift(peak, phase, ROWS, k)) for k in (1, 2, 3)]:
             peak = jnp.maximum(peak, other)
-        home = [sent[0]] + [shift(sent[j], phase, "columns", -j) for j in (1, 2, 3)]
-        peaks = jnp.stack([peak] + [shift(peak, phase, "columns", -j) for j in (1, 2, 3)])
+        home = [sent[0]] + [shift(sent[j], phase, COLUMNS, -j) for j in (1, 2, 3)]
+        peaks = jnp.stack([peak] + [shift(peak, phase, COLUMNS, -j) for j in (1, 2, 3)])
         return home, peaks
 
     tokens = call(
@@ -674,7 +727,7 @@
 
     total_rows = SIDE * SIDE * rows
     part = span // SIDE
-    gathered_specs = [everything, everything, half, half, everything]
+    gathered_specs = [half] * (2 * SIDE)
     tall = pl.BlockSpec((span, part), lambda i, ids: (0, 0))
     small = pl.BlockSpec((part, part), lambda i, ids: (0, 0))
     flipped = pl.BlockSpec((span, total_rows), lambda i, ids: (0, 0))
@@ -695,9 +748,10 @@
         [flipped, *gathered_specs],
         [jax.ShapeDtypeStruct((span, part), bf16)] * SIDE,
         [tall] * SIDE,
+        [pltpu.VMEM((SIDE, span, part), bf16)],
         flops=2 * total_rows * span * span,
     )
-    arrived = [partials[0]] + [ring(partials[k], "dp", k) for k in (1, 2, 3)]
+    arrived = [partials[0]] + [ring(partials[k], DP, k) for k in (1, 2, 3)]
     pieces = call(
         total_body,
         ids,
@@ -707,7 +761,7 @@
         [jax.ShapeDtypeStruct((part, part), bf16)] * SIDE,
         [small] * SIDE,
     )
-    pieces = [pieces[0]] + [ring(pieces[k], "tensor_1", k) for k in (1, 2, 3)]
+    pieces = [pieces[0]] + [ring(pieces[k], FAST, k) for k in (1, 2, 3)]
     pieces = call(
         choose_body,
         ids,
@@ -717,7 +771,7 @@
         [jax.ShapeDtypeStruct((part, part), bf16)] * SIDE,
         [small] * SIDE,
     )
-    pieces = [pieces[0]] + [ring(pieces[k], "dp", k) for k in (1, 2, 3)]
+    pieces = [pieces[0]] + [ring(pieces[k], DP, k) for k in (1, 2, 3)]
     weight_grad = call(
         finish_body,
         ids,
@@ -732,23 +786,23 @@
 
 def solution(mesh):
     finer = Mesh(
-        mesh.devices.reshape(mesh.shape["dp"], mesh.shape["section"], SIDE, SIDE),
-        ("dp", "section", "tensor_0", "tensor_1"),
+        mesh.devices.reshape(mesh.shape[DP], mesh.shape[SECTION], SIDE, SIDE),
+        (DP, SECTION, "tensor_0", FAST),
     )
     return jax.shard_map(
         local,
         mesh=finer,
         in_specs=(
             P(None, DP_TENSOR, None),
-            P("section", TENSOR, None),
-            P("section", None, None, DP_TENSOR, None),
-            P("section", None, None, "dp", None),
+            P(SECTION, TENSOR, None),
+            P(SECTION, None, None, DP_TENSOR, None),
+            P(SECTION, None, None, DP, None),
             P(None, DP_TENSOR, None),
         ),
         out_specs=(
-            P("section", None, DP_TENSOR, None),
-            P("section", None, DP_TENSOR, None),
-            P("section", TENSOR, "dp"),
+            P(SECTION, None, DP_TENSOR, None),
+            P(SECTION, None, DP_TENSOR, None),
+            P(SECTION, TENSOR, DP),
         ),
         check_vma=False,
     )

time: 265 us -> 255 us (0.962)
  waiting for transfers between devices: 136 us -> 90.1 us
  starting transfers between devices: 67.1 us -> 103 us
  Pallas kernels: 52.9 us -> 57.8 us
  local copies, waits for them, and re-layouts: 5.66 us -> 1.77 us
    ppermute x44 -> x54, waiting for transfers between devices: 99.8 us -> 64.9 us  [shift(): return lax.ppermute(value, CHIP, pairs)]
    ppermute x44 -> x54, starting transfers between devices: 47 us -> 79.6 us  [shift(): return lax.ppermute(value, CHIP, pairs)]
    ppermute x14, waiting for transfers between devices: 35.3 us -> 23.8 us  [ring(): lax.ppermute(value, axis, [(i, (i + steps) % SIDE) for i in range(SIDE)])]
    pallas_call x18 -> x20, Pallas kernels: 52.9 us -> 57.8 us  [call(): pl.pallas_call(body, grid_spec=pltpu.PrefetchScalarGridSpec(num_scalar_pr...]
    unnamed x18 -> x10, local copies, waits for them, and re-layouts: 5.36 us -> 1.61 us
    ppermute x14, starting transfers between devices: 19.1 us -> 22.2 us  [ring(): lax.ppermute(value, axis, [(i, (i + steps) % SIDE) for i in range(SIDE)])]
  transfers between devices with their start and end apart: 63 -> 73, of which waited for: 28 -> 28; matrix products, arithmetic and copies ran while one was open for 0% -> 0% of each run, Pallas kernels for 11% -> 14%
where the time goes in v1:
time: 255 us; the launch traced here: 254 us
  starting transfers between devices  103 us (40%)
  waiting for transfers between devices  90.1 us (35%)
  Pallas kernels  57.8 us (23%)
    ppermute x54, starting transfers between devices, shift(): return lax.ppermute(value, CHIP, pairs)  79.6 us
    ppermute x54, waiting for transfers between devices, shift(): return lax.ppermute(value, CHIP, pairs)  64.9 us
    pallas_call x20, Pallas kernels, call(): pl.pallas_call(body, grid_spec=pltpu.PrefetchScalarGridSpec(num_scalar_pr...  57.8 us
    ppermute x14, waiting for transfers between devices, ring(): lax.ppermute(value, axis, [(i, (i + steps) % SIDE) for i in range(SIDE)])  23.8 us
    ppermute x14, starting transfers between devices, ring(): lax.ppermute(value, axis, [(i, (i + steps) % SIDE) for i in range(SIDE)])  22.2 us
  transfers between devices with their start and end apart: 73, of which 28 were waited for; matrix products, arithmetic and copies ran while one was open for 0% of the time, Pallas kernels for 14%

profile of v1, /device:TPU:0, one launch (start us, length us, event | category | flops | bytes accessed | tf_op | source)
XLA Modules:
  0.0 254.2 jit_solution(4486951148058053791)
XLA Ops:
  13.6 3.6 %collective-permute-start.1 = (bf16[128,1024]{1,0:T(8,128)(2,1)S(1)}, bf16[128,1024]{1,0:T(8,128)(2,1)S(1)}, u32[]{:S(2)}, u32[]{:S(2)}) collective-permute-start(bf16[128,1024]{1,0:T(8,128)(2,1)S(1)} %get-tuple-element.79), channel_id=1, source_target_pairs={{0,8},{1,9},{2,10},{3,11},{4,12},{5,13},{6,14},{7,15},{8,0},{9,1},... | collective-permute-start | bytes 786440 | tf_op jit(solution)/shard_map/ppermute | solution.py:49
  33.5 4.1 %collective-permute-start.5 = (bf16[2,128,1024]{2,1,0:T(8,128)(2,1)S(1)}, bf16[2,128,1024]{2,1,0:T(8,128)(2,1)S(1)}, u32[]{:S(2)}, u32[]{:S(2)}) collective-permute-start(bf16[2,128,1024]{2,1,0:T(8,128)(2,1)S(1)} %pad_maximum_fusion.refs_0_), channel_id=1, source_target_pairs={{0,3},{1,0},{2,1},{3,2},{4,7},{5,4},{6,5},{7,6},{8,11},{9,8},{10,9... | collective-permute-start | bytes 1572872 | tf_op jit(solution)/shard_map/ppermute | solution.py:49
  44.4 6.0 %shard_map.79 = (bf16[2,128,1024]{2,1,0:T(8,128)(2,1)S(1)}, bf16[2,128,1024]{2,1,0:T(8,128)(2,1)S(1)}, bf16[2,128,1024]{2,1,0:T(8,128)(2,1)S(1)}, bf16[2,128,102...) custom-call(s32[7]{0:T(128)S(1)} %stack.121.ids, ...), custom_call_target="tpu_custom_call" | custom-call | flops 3221225472 | bytes 8000000 | tf_op jit(solution)/shard_map/pallas_call | solution.py:70
  50.4 4.2 %collective-permute-start.12 = (bf16[2,128,1024]{2,1,0:T(8,128)(2,1)S(1)}, bf16[2,128,1024]{2,1,0:T(8,128)(2,1)S(1)}, u32[]{:S(2)}, u32[]{:S(2)}) collective-permute-start(bf16[2,128,1024]{2,1,0:T(8,128)(2,1)S(1)} %get-tuple-element.87), channel_id=1, source_target_pairs={{0,12},{1,13},{2,14},{3,15},{4,0},{5,1},{6,2},{7,3},{8,4},{9,5},{1... | collective-permute-start | bytes 1572872 | tf_op jit(solution)/shard_map/ppermute | solution.py:49
  57.0 4.2 %shard_map.82 = (bf16[128,1024]{1,0:T(8,128)(2,1)S(1)}, bf16[128,1024]{1,0:T(8,128)(2,1)S(1)}, bf16[128,1024]{1,0:T(8,128)(2,1)S(1)}, bf16[128,1024]{1,0:T(8,128)(2,1)S(1)}) custom-call(s32[7]{0:T(128)S(1)} %stack.121.ids, f32[2,8,32]{2,1,0:T(8,128)S(1)} %bitcast.67, s32[2,8,16,4096]{3,2,1,0:T(8,128)S(1)} %bitcast.54, s32[2,8,16,4096]{3,2,1,0:T(8,128)S(1)} %bitcast.55, ...), custom_call_target="tpu_custom_call" | custom-call | flops 20000000 | bytes 8000000 | tf_op jit(solution)/shard_map/pallas_call | solution.py:70
  61.3 5.1 %collective-permute-start.21 = (bf16[128,1024]{1,0:T(8,128)(2,1)S(1)}, bf16[128,1024]{1,0:T(8,128)(2,1)S(1)}, u32[]{:S(2)}, u32[]{:S(2)}) collective-permute-start(bf16[128,1024]{1,0:T(8,128)(2,1)S(1)} %get-tuple-element.101), channel_id=1, source_target_pairs={{0,2},{1,3},{2,0},{3,1},{4,6},{5,7},{6,4},{7,5},{8,10},{9,11},{10,... | collective-permute-start | bytes 786440 | tf_op jit(solution)/shard_map/ppermute | solution.py:49
  66.5 3.2 %collective-permute-start.18 = (bf16[2,128,1024]{2,1,0:T(8,128)(2,1)S(1)}, bf16[2,128,1024]{2,1,0:T(8,128)(2,1)S(1)}, u32[]{:S(2)}, u32[]{:S(2)}) collective-permute-start(bf16[2,128,1024]{2,1,0:T(8,128)(2,1)S(1)} %get-tuple-element.97), channel_id=1, source_target_pairs={{0,12},{1,13},{2,14},{3,15},{4,0},{5,1},{6,2},{7,3},{8,4},{9,5},{1... | collective-permute-start | bytes 1572872 | tf_op jit(solution)/shard_map/ppermute | solution.py:49
  75.3 3.9 %collective-permute-done.21.o2 = bf16[128,1024]{1,0:T(8,128)(2,1)S(1)} collective-permute-done((bf16[128,1024]{1,0:T(8,128)(2,1)S(1)}, bf16[128,1024]{1,0:T(8,128)(2,1)S(1)}, u32[]{:S(2)}, u32[]{:S(2)}) %collective-permute-start.21) | collective-permute-done | bytes 262176 | tf_op jit(solution)/shard_map/ppermute | solution.py:49
  79.2 6.4 %collective-permute-done.22.o3 = bf16[128,1024]{1,0:T(8,128)(2,1)S(1)} collective-permute-done((bf16[128,1024]{1,0:T(8,128)(2,1)S(1)}, bf16[128,1024]{1,0:T(8,128)(2,1)S(1)}, u32[]{:S(2)}, u32[]{:S(2)}) %collective-permute-start.22) | collective-permute-done | bytes 262176 | tf_op jit(solution)/shard_map/ppermute | solution.py:49
  100.8 3.5 %collective-permute-done.35 = f32[8,1,1024]{2,1,0:T(1,128)S(1)} collective-permute-done((f32[8,1,1024]{2,1,0:T(1,128)S(1)}, f32[8,1,1024]{2,1,0:T(1,128)S(1)}, u32[]{:S(2)}, u32[]{:S(2)}) %collective-permute-start.35) | collective-permute-done | bytes 32800 | tf_op jit(solution)/shard_map/ppermute | solution.py:49
  109.8 6.4 %shard_map.84 = (bf16[128,1024]{1,0:T(8,128)(2,1)S(1)}, bf16[128,1024]{1,0:T(8,128)(2,1)S(1)}, bf16[128,1024]{1,0:T(8,128)(2,1)S(1)}, bf16[128,1024]{1,0:T(8,128)(2,1)S(1)}, bf16[8,16,4096]{2,1,0:T(8,128)(2,1)S(1)}) custom-call(s32[7]{0:T(128)S(1)} %stack.121.ids, f32[2,8,32]{2,1,0:T(8,128)S(1)} %bitcast.68, ...), custom_call_target="tpu_custom_call" | custom-call | flops 20000000 | bytes 8000000 | tf_op jit(solution)/shard_map/pallas_call | solution.py:70
  119.0 5.3 %collective-permute-done.38 = bf16[128,1024]{1,0:T(8,128)(2,1)S(1)} collective-permute-done((bf16[128,1024]{1,0:T(8,128)(2,1)S(1)}, bf16[128,1024]{1,0:T(8,128)(2,1)S(1)}, u32[]{:S(2)}, u32[]{:S(2)}) %collective-permute-start.38) | collective-permute-done | bytes 262176 | tf_op jit(solution)/shard_map/ppermute | solution.py:49
  136.0 3.4 %collective-permute-start.46 = (bf16[2,128,1024]{2,1,0:T(8,128)(2,1)S(1)}, bf16[2,128,1024]{2,1,0:T(8,128)(2,1)S(1)}, u32[]{:S(2)}, u32[]{:S(2)}) collective-permute-start(bf16[2,128,1024]{2,1,0:T(8,128)(2,1)S(1)} %collective-permute-done.43.refs_5_.refs_7_), channel_id=1, source_target_pairs={{0,12},{1,13},{2,14},{3,15},{4,0},{5,1},{6,2},{7,3},{8,4},{9,5},{1... | collective-permute-start | bytes 1572872 | tf_op jit(solution)/shard_map/ppermute | solution.py:49
  147.3 3.6 %collective-permute-done.45.low.refs_4_ = bf16[2,128,1024]{2,1,0:T(8,128)(2,1)S(1)} collective-permute-done((bf16[2,128,1024]{2,1,0:T(8,128)(2,1)S(1)}, bf16[2,128,1024]{2,1,0:T(8,128)(2,1)S(1)}, u32[]{:S(2)}, u32[]{:S(2)}) %collective-permute-start.45) | collective-permute-done | bytes 524320 | tf_op jit(solution)/shard_map/ppermute | solution.py:49
  150.8 8.1 %shard_map.92 = (bf16[1024,256]{1,0:T(8,128)(2,1)S(1)}, bf16[1024,256]{1,0:T(8,128)(2,1)S(1)}, bf16[1024,256]{1,0:T(8,128)(2,1)S(1)}, bf16[1024,256]{1,0:T(8,128)(2,1)S(1)}) custom-call(s32[7]{0:T(128)S(1)} %stack.121.ids, bf16[1024,2048]{1,0:T(8,128)(2,1)S(1)} %shard_map.91.left, bf16[2,128,1024]{2,1,0:T(8,128)(2,1)S(1)} %pad_maximum_fusion.4.refs_0_, ...), custom_call_target="tpu_custom_call" | custom-call | flops 4294967296 | bytes 8000000 | tf_op jit(solution)/shard_map/pallas_call | solution.py:70
  163.4 6.5 %shard_map.85 = (bf16[2,128,1024]{2,1,0:T(8,128)(2,1)S(1)}, bf16[2,128,1024]{2,1,0:T(8,128)(2,1)S(1)}, bf16[2,128,1024]{2,1,0:T(8,128)(2,1)S(1)}, bf16[2,128,102...) custom-call(s32[7]{0:T(128)S(1)} %stack.121.ids, ...), custom_call_target="tpu_custom_call" | custom-call | flops 3221225472 | bytes 8000000 | tf_op jit(solution)/shard_map/pallas_call | solution.py:70
  177.0 6.2 %collective-permute-done.64.q1 = bf16[1024,256]{1,0:T(8,128)(2,1)S(1)} collective-permute-done((bf16[1024,256]{1,0:T(8,128)(2,1)S(1)}, bf16[1024,256]{1,0:T(8,128)(2,1)S(1)}, u32[]{:S(2)}, u32[]{:S(2)}) %collective-permute-start.64) | collective-permute-done | bytes 524320 | tf_op jit(solution)/shard_map/ppermute | solution.py:53
  189.9 5.4 %collective-permute-done.47.b1 = bf16[2,128,1024]{2,1,0:T(8,128)(2,1)S(1)} collective-permute-done((bf16[2,128,1024]{2,1,0:T(8,128)(2,1)S(1)}, bf16[2,128,1024]{2,1,0:T(8,128)(2,1)S(1)}, u32[]{:S(2)}, u32[]{:S(2)}) %collective-permute-start.47) | collective-permute-done | bytes 524320 | tf_op jit(solution)/shard_map/ppermute | solution.py:49
  196.2 3.3 %collective-permute-start.50 = (bf16[2,128,1024]{2,1,0:T(8,128)(2,1)S(1)}, bf16[2,128,1024]{2,1,0:T(8,128)(2,1)S(1)}, u32[]{:S(2)}, u32[]{:S(2)}) collective-permute-start(bf16[2,128,1024]{2,1,0:T(8,128)(2,1)S(1)} %get-tuple-element.124), channel_id=1, source_target_pairs={{0,3},{1,0},{2,1},{3,2},{4,7},{5,4},{6,5},{7,6},{8,11},{9,8},{10,9... | collective-permute-start | bytes 1572872 | tf_op jit(solution)/shard_map/ppermute | solution.py:49
  202.8 13.2 %collective-permute-done.69.r3 = bf16[256,256]{1,0:T(8,128)(2,1)S(1)} collective-permute-done((bf16[256,256]{1,0:T(8,128)(2,1)S(1)}, bf16[256,256]{1,0:T(8,128)(2,1)S(1)}, u32[]{:S(2)}, u32[]{:S(2)}) %collective-permute-start.69) | collective-permute-done | bytes 131104 | tf_op jit(solution)/shard_map/ppermute | solution.py:53
  216.7 5.7 %collective-permute-done.54.o3 = bf16[128,1024]{1,0:T(8,128)(2,1)S(1)} collective-permute-done((bf16[128,1024]{1,0:T(8,128)(2,1)S(1)}, bf16[128,1024]{1,0:T(8,128)(2,1)S(1)}, u32[]{:S(2)}, u32[]{:S(2)}) %collective-permute-start.54) | collective-permute-done | bytes 262176 | tf_op jit(solution)/shard_map/ppermute | solution.py:49
  224.9 3.7 %collective-permute-start.60 = (f32[8,1,1024]{2,1,0:T(1,128)S(1)}, f32[8,1,1024]{2,1,0:T(1,128)S(1)}, u32[]{:S(2)}, u32[]{:S(2)}) collective-permute-start(f32[8,1,1024]{2,1,0:T(1,128)S(1)} %get-tuple-element.135), channel_id=1, source_target_pairs={{0,3},{1,0},{2,1},{3,2},{4,7},{5,4},{6,5},{7,6},{8,11},{9,8},{10,9... | collective-permute-start | bytes 98312 | tf_op jit(solution)/shard_map/ppermute | solution.py:49
  239.8 5.8 %collective-permute-done.63 = f32[8,1,1024]{2,1,0:T(1,128)S(1)} collective-permute-done((f32[8,1,1024]{2,1,0:T(1,128)S(1)}, f32[8,1,1024]{2,1,0:T(1,128)S(1)}, u32[]{:S(2)}, u32[]{:S(2)}) %collective-permute-start.63) | collective-permute-done | bytes 32800 | tf_op jit(solution)/shard_map/ppermute | solution.py:49
  249.7 4.4 %shard_map.90 = (bf16[8,16,4096]{2,1,0:T(8,128)(2,1)}, bf16[8,16,4096]{2,1,0:T(8,128)(2,1)}) custom-call(s32[7]{0:T(128)S(1)} %stack.121.ids, f32[2,8,32]{2,1,0:T(8,128)S(1)} %bitcast.70, bf16[128,1024]{1,0:T(8,128)(2,1)S(1)} %get-tuple-element.131.r0, bf16[128,1024]{1,0:T(8,128)(2,1)S(1)} %collective-permute-done.55.r1, ...), custom_call_target="tpu_custom_call" | custom-call | flops 20000000 | bytes 8000000 | tf_op jit(solution)/shard_map/pallas_call | solution.py:70
  (167 shorter events, 127.7 us)
Async XLA Ops:
  3.0 14.2 %collective-permute-start.7 = (bf16[128,1024]{1,0:T(8,128)(2,1)S(1)}, bf16[128,1024]{1,0:T(8,128)(2,1)S(1)}, u32[]{:S(2)}, u32[]{:S(2)}) collective-permute-start(bf16[128,1024]{1,0:T(8,128)(2,1)S(1)} %get-tuple-element.82), channel_id=1, source_target_pairs={{0,1},{1,2},{2,3},{3,0},{4,5},{5,6},{6,7},{7,4},{8,9},{9,10},{10,1... | collective-permute-start | bytes 786440 | tf_op jit(solution)/shard_map/ppermute | solution.py:53
  4.7 15.7 %collective-permute-start.8 = (bf16[128,1024]{1,0:T(8,128)(2,1)S(1)}, bf16[128,1024]{1,0:T(8,128)(2,1)S(1)}, u32[]{:S(2)}, u32[]{:S(2)}) collective-permute-start(bf16[128,1024]{1,0:T(8,128)(2,1)S(1)} %get-tuple-element.83), channel_id=1, source_target_pairs={{0,2},{1,3},{2,0},{3,1},{4,6},{5,7},{6,4},{7,5},{8,10},{9,11},{10,... | collective-permute-start | bytes 786440 | tf_op jit(solution)/shard_map/ppermute | solution.py:53
  37.7 16.9 %collective-permute-start.14 = (bf16[2,128,1024]{2,1,0:T(8,128)(2,1)S(1)}, bf16[2,128,1024]{2,1,0:T(8,128)(2,1)S(1)}, u32[]{:S(2)}, u32[]{:S(2)}) collective-permute-start(bf16[2,128,1024]{2,1,0:T(8,128)(2,1)S(1)} %collective-permute-done.6.refs_5_.refs_7_), channel_id=1, source_target_pairs={{0,3},{1,0},{2,1},{3,2},{4,7},{5,4},{6,5},{7,6},{8,11},{9,8},{10,9... | collective-permute-start | bytes 1572872 | tf_op jit(solution)/shard_map/ppermute | solution.py:49
  37.7 16.9 %collective-permute-start.13 = (bf16[2,128,1024]{2,1,0:T(8,128)(2,1)S(1)}, bf16[2,128,1024]{2,1,0:T(8,128)(2,1)S(1)}, u32[]{:S(2)}, u32[]{:S(2)}) collective-permute-start(bf16[2,128,1024]{2,1,0:T(8,128)(2,1)S(1)} %collective-permute-done.3.refs_2_), channel_id=1, source_target_pairs={{0,1},{1,2},{2,3},{3,0},{4,5},{5,6},{6,7},{7,4},{8,9},{9,10},{10,1... | collective-permute-start | bytes 1572872 | tf_op jit(solution)/shard_map/ppermute | solution.py:49
  50.4 16.1 %collective-permute-start.12 = (bf16[2,128,1024]{2,1,0:T(8,128)(2,1)S(1)}, bf16[2,128,1024]{2,1,0:T(8,128)(2,1)S(1)}, u32[]{:S(2)}, u32[]{:S(2)}) collective-permute-start(bf16[2,128,1024]{2,1,0:T(8,128)(2,1)S(1)} %get-tuple-element.87), channel_id=1, source_target_pairs={{0,12},{1,13},{2,14},{3,15},{4,0},{5,1},{6,2},{7,3},{8,4},{9,5},{1... | collective-permute-start | bytes 1572872 | tf_op jit(solution)/shard_map/ppermute | solution.py:49
  56.9 15.4 %collective-permute-start.15 = (bf16[2,128,1024]{2,1,0:T(8,128)(2,1)S(1)}, bf16[2,128,1024]{2,1,0:T(8,128)(2,1)S(1)}, u32[]{:S(2)}, u32[]{:S(2)}) collective-permute-start(bf16[2,128,1024]{2,1,0:T(8,128)(2,1)S(1)} %get-tuple-element.93), channel_id=1, source_target_pairs={{0,4},{1,5},{2,6},{3,7},{4,8},{5,9},{6,10},{7,11},{8,12},{9,13},{1... | collective-permute-start | bytes 1572872 | tf_op jit(solution)/shard_map/ppermute | solution.py:49
  61.3 17.9 %collective-permute-start.21 = (bf16[128,1024]{1,0:T(8,128)(2,1)S(1)}, bf16[128,1024]{1,0:T(8,128)(2,1)S(1)}, u32[]{:S(2)}, u32[]{:S(2)}) collective-permute-start(bf16[128,1024]{1,0:T(8,128)(2,1)S(1)} %get-tuple-element.101), channel_id=1, source_target_pairs={{0,2},{1,3},{2,0},{3,1},{4,6},{5,7},{6,4},{7,5},{8,10},{9,11},{10,... | collective-permute-start | bytes 786440 | tf_op jit(solution)/shard_map/ppermute | solution.py:49
  66.5 19.1 %collective-permute-start.17 = (bf16[2,128,1024]{2,1,0:T(8,128)(2,1)S(1)}, bf16[2,128,1024]{2,1,0:T(8,128)(2,1)S(1)}, u32[]{:S(2)}, u32[]{:S(2)}) collective-permute-start(bf16[2,128,1024]{2,1,0:T(8,128)(2,1)S(1)} %get-tuple-element.95), channel_id=1, source_target_pairs={{0,4},{1,5},{2,6},{3,7},{4,8},{5,9},{6,10},{7,11},{8,12},{9,13},{1... | collective-permute-start | bytes 1572872 | tf_op jit(solution)/shard_map/ppermute | solution.py:49
  66.5 19.1 %collective-permute-start.18 = (bf16[2,128,1024]{2,1,0:T(8,128)(2,1)S(1)}, bf16[2,128,1024]{2,1,0:T(8,128)(2,1)S(1)}, u32[]{:S(2)}, u32[]{:S(2)}) collective-permute-start(bf16[2,128,1024]{2,1,0:T(8,128)(2,1)S(1)} %get-tuple-element.97), channel_id=1, source_target_pairs={{0,12},{1,13},{2,14},{3,15},{4,0},{5,1},{6,2},{7,3},{8,4},{9,5},{1... | collective-permute-start | bytes 1572872 | tf_op jit(solution)/shard_map/ppermute | solution.py:49
  129.6 15.6 %collective-permute-start.41 = (bf16[2,128,1024]{2,1,0:T(8,128)(2,1)S(1)}, bf16[2,128,1024]{2,1,0:T(8,128)(2,1)S(1)}, u32[]{:S(2)}, u32[]{:S(2)}) collective-permute-start(bf16[2,128,1024]{2,1,0:T(8,128)(2,1)S(1)} %pad_maximum_fusion.5.refs_1_), channel_id=1, source_target_pairs={{0,4},{1,5},{2,6},{3,7},{4,8},{5,9},{6,10},{7,11},{8,12},{9,13},{1... | collective-permute-start | bytes 1572872 | tf_op jit(solution)/shard_map/ppermute | solution.py:49
  158.9 24.3 %collective-permute-start.64 = (bf16[1024,256]{1,0:T(8,128)(2,1)S(1)}, bf16[1024,256]{1,0:T(8,128)(2,1)S(1)}, u32[]{:S(2)}, u32[]{:S(2)}) collective-permute-start(bf16[1024,256]{1,0:T(8,128)(2,1)S(1)} %get-tuple-element.140), channel_id=1, source_target_pairs={{0,32},{32,64},{64,96},{96,0},{1,33},{33,65},{65,97},{97,1},{2,34}... | collective-permute-start | bytes 1572872 | tf_op jit(solution)/shard_map/ppermute | solution.py:53
  159.3 25.4 %collective-permute-start.65 = (bf16[1024,256]{1,0:T(8,128)(2,1)S(1)}, bf16[1024,256]{1,0:T(8,128)(2,1)S(1)}, u32[]{:S(2)}, u32[]{:S(2)}) collective-permute-start(bf16[1024,256]{1,0:T(8,128)(2,1)S(1)} %get-tuple-element.141), channel_id=1, source_target_pairs={{0,64},{32,96},{64,0},{96,32},{1,65},{33,97},{65,1},{97,33},{2,66}... | collective-permute-start | bytes 1572872 | tf_op jit(solution)/shard_map/ppermute | solution.py:53
  162.0 25.4 %collective-permute-start.66 = (bf16[1024,256]{1,0:T(8,128)(2,1)S(1)}, bf16[1024,256]{1,0:T(8,128)(2,1)S(1)}, u32[]{:S(2)}, u32[]{:S(2)}) collective-permute-start(bf16[1024,256]{1,0:T(8,128)(2,1)S(1)} %get-tuple-element.142), channel_id=1, source_target_pairs={{0,96},{32,0},{64,32},{96,64},{1,97},{33,1},{65,33},{97,65},{2,98}... | collective-permute-start | bytes 1572872 | tf_op jit(solution)/shard_map/ppermute | solution.py:53
  170.0 18.3 %collective-permute-start.44 = (bf16[2,128,1024]{2,1,0:T(8,128)(2,1)S(1)}, bf16[2,128,1024]{2,1,0:T(8,128)(2,1)S(1)}, u32[]{:S(2)}, u32[]{:S(2)}) collective-permute-start(bf16[2,128,1024]{2,1,0:T(8,128)(2,1)S(1)} %get-tuple-element.114), channel_id=1, source_target_pairs={{0,3},{1,0},{2,1},{3,2},{4,7},{5,4},{6,5},{7,6},{8,11},{9,8},{10,9... | collective-permute-start | bytes 1572872 | tf_op jit(solution)/shard_map/ppermute | solution.py:49
  175.1 20.1 %collective-permute-start.47 = (bf16[2,128,1024]{2,1,0:T(8,128)(2,1)S(1)}, bf16[2,128,1024]{2,1,0:T(8,128)(2,1)S(1)}, u32[]{:S(2)}, u32[]{:S(2)}) collective-permute-start(bf16[2,128,1024]{2,1,0:T(8,128)(2,1)S(1)} %get-tuple-element.120), channel_id=1, source_target_pairs={{0,1},{1,2},{2,3},{3,0},{4,5},{5,6},{6,7},{7,4},{8,9},{9,10},{10,1... | collective-permute-start | bytes 1572872 | tf_op jit(solution)/shard_map/ppermute | solution.py:49
  184.7 14.8 %collective-permute-start.53 = (bf16[128,1024]{1,0:T(8,128)(2,1)S(1)}, bf16[128,1024]{1,0:T(8,128)(2,1)S(1)}, u32[]{:S(2)}, u32[]{:S(2)}) collective-permute-start(bf16[128,1024]{1,0:T(8,128)(2,1)S(1)} %get-tuple-element.129), channel_id=1, source_target_pairs={{0,8},{1,9},{2,10},{3,11},{4,12},{5,13},{6,14},{7,15},{8,0},{9,1},... | collective-permute-start | bytes 786440 | tf_op jit(solution)/shard_map/ppermute | solution.py:49
  195.3 27.6 %collective-permute-start.49 = (bf16[2,128,1024]{2,1,0:T(8,128)(2,1)S(1)}, bf16[2,128,1024]{2,1,0:T(8,128)(2,1)S(1)}, u32[]{:S(2)}, u32[]{:S(2)}) collective-permute-start(bf16[2,128,1024]{2,1,0:T(8,128)(2,1)S(1)} %get-tuple-element.122), channel_id=1, source_target_pairs={{0,1},{1,2},{2,3},{3,0},{4,5},{5,6},{6,7},{7,4},{8,9},{9,10},{10,1... | collective-permute-start | bytes 1572872 | tf_op jit(solution)/shard_map/ppermute | solution.py:49
  196.2 26.8 %collective-permute-start.50 = (bf16[2,128,1024]{2,1,0:T(8,128)(2,1)S(1)}, bf16[2,128,1024]{2,1,0:T(8,128)(2,1)S(1)}, u32[]{:S(2)}, u32[]{:S(2)}) collective-permute-start(bf16[2,128,1024]{2,1,0:T(8,128)(2,1)S(1)} %get-tuple-element.124), channel_id=1, source_target_pairs={{0,3},{1,0},{2,1},{3,2},{4,7},{5,4},{6,5},{7,6},{8,11},{9,8},{10,9... | collective-permute-start | bytes 1572872 | tf_op jit(solution)/shard_map/ppermute | solution.py:49
  199.5 23.4 %collective-permute-start.48 = (bf16[2,128,1024]{2,1,0:T(8,128)(2,1)S(1)}, bf16[2,128,1024]{2,1,0:T(8,128)(2,1)S(1)}, u32[]{:S(2)}, u32[]{:S(2)}) collective-permute-start(bf16[2,128,1024]{2,1,0:T(8,128)(2,1)S(1)} %get-tuple-element.121), channel_id=1, source_target_pairs={{0,3},{1,0},{2,1},{3,2},{4,7},{5,4},{6,5},{7,6},{8,11},{9,8},{10,9... | collective-permute-start | bytes 1572872 | tf_op jit(solution)/shard_map/ppermute | solution.py:49
  199.6 23.4 %collective-permute-start.51 = (bf16[2,128,1024]{2,1,0:T(8,128)(2,1)S(1)}, bf16[2,128,1024]{2,1,0:T(8,128)(2,1)S(1)}, u32[]{:S(2)}, u32[]{:S(2)}) collective-permute-start(bf16[2,128,1024]{2,1,0:T(8,128)(2,1)S(1)} %get-tuple-element.125), channel_id=1, source_target_pairs={{0,1},{1,2},{2,3},{3,0},{4,5},{5,6},{6,7},{7,4},{8,9},{9,10},{10,1... | collective-permute-start | bytes 1572872 | tf_op jit(solution)/shard_map/ppermute | solution.py:49
  201.5 14.5 %collective-permute-start.69 = (bf16[256,256]{1,0:T(8,128)(2,1)S(1)}, bf16[256,256]{1,0:T(8,128)(2,1)S(1)}, u32[]{:S(2)}, u32[]{:S(2)}) collective-permute-start(bf16[256,256]{1,0:T(8,128)(2,1)S(1)} %get-tuple-element.146), channel_id=1, source_target_pairs={{0,3},{1,0},{2,1},{3,2},{4,7},{5,4},{6,5},{7,6},{8,11},{9,8},{10,9... | collective-permute-start | bytes 393224 | tf_op jit(solution)/shard_map/ppermute | solution.py:53
  233.4 16.3 %collective-permute-start.55 = (bf16[128,1024]{1,0:T(8,128)(2,1)S(1)}, bf16[128,1024]{1,0:T(8,128)(2,1)S(1)}, u32[]{:S(2)}, u32[]{:S(2)}) collective-permute-start(bf16[128,1024]{1,0:T(8,128)(2,1)S(1)} %get-tuple-element.132), channel_id=1, source_target_pairs={{0,12},{1,13},{2,14},{3,15},{4,0},{5,1},{6,2},{7,3},{8,4},{9,5},{1... | collective-permute-start | bytes 786440 | tf_op jit(solution)/shard_map/ppermute | solution.py:49
  234.6 15.1 %collective-permute-start.56 = (bf16[128,1024]{1,0:T(8,128)(2,1)S(1)}, bf16[128,1024]{1,0:T(8,128)(2,1)S(1)}, u32[]{:S(2)}, u32[]{:S(2)}) collective-permute-start(bf16[128,1024]{1,0:T(8,128)(2,1)S(1)} %get-tuple-element.133), channel_id=1, source_target_pairs={{0,8},{1,9},{2,10},{3,11},{4,12},{5,13},{6,14},{7,15},{8,0},{9,1},... | collective-permute-start | bytes 786440 | tf_op jit(solution)/shard_map/ppermute | solution.py:49
  235.0 14.7 %collective-permute-start.57 = (bf16[128,1024]{1,0:T(8,128)(2,1)S(1)}, bf16[128,1024]{1,0:T(8,128)(2,1)S(1)}, u32[]{:S(2)}, u32[]{:S(2)}) collective-permute-start(bf16[128,1024]{1,0:T(8,128)(2,1)S(1)} %get-tuple-element.134), channel_id=1, source_target_pairs={{0,4},{1,5},{2,6},{3,7},{4,8},{5,9},{6,10},{7,11},{8,12},{9,13},{1... | collective-permute-start | bytes 786440 | tf_op jit(solution)/shard_map/ppermute | solution.py:49
  (54 other events, 479.4 us)
